TPU v7x, 256 devices: a whole 4x4x8 slice. The times are simulated.
256 devices in a mesh: col: 4 (over x), row: 64 (over z, y, core).
Axes of the slice: x: 4, y: 4, z: 8, core: 2. Of those that a mesh axis runs over, the one named last changes fastest.
Arguments:
- inter_mask: int32 [65536, 4096], P('row', 'col')
- emb_user: bfloat16 [65536, 64], P(('row', 'col'))
- emb_item: bfloat16 [4096, 64], P(('col', 'row'))
- triples: int32 [1024, 3], replicated
Outputs:
- output 1: bfloat16 [65536, 64], P(('row', 'col'))
- output 2: bfloat16 [4096, 64], P(('col', 'row'))
- output 3: float32 [1024], replicated
All inputs are finite; a program needn't handle non-finite values.
Results may differ from a plain program's by a relative error of at most 0.00555861.
Values are sent between devices in bfloat16 or wider.
A program may use at most 768 MiB of HBM per device.

v0:
```python
import jax
import jax.numpy as jnp
from jax import lax
from jax.sharding import PartitionSpec as P

LAYERS = 3


def solution(mesh):
    row_count = mesh.shape["row"]
    col_count = mesh.shape["col"]

    def lookup(emb_table, row_ids, row_start):
        local_ids = row_ids - row_start
        is_owned = (local_ids >= 0) & (local_ids < emb_table.shape[0])
        rows_got = jnp.take(emb_table, jnp.clip(local_ids, 0, emb_table.shape[0] - 1), axis=0).astype(jnp.float32)
        return jnp.where(is_owned[:, None], rows_got, 0.0)

    def device_body(mask_blk, user_shard, item_shard, triples):
        row_idx = lax.axis_index("row")
        col_idx = lax.axis_index("col")
        deg_user = lax.psum(jnp.sum(mask_blk, axis=1), "col")
        deg_item = lax.psum(jnp.sum(mask_blk, axis=0), "row")
        scale_user = lax.rsqrt(jnp.maximum(deg_user, 1).astype(jnp.float32))
        scale_item = lax.rsqrt(jnp.maximum(deg_item, 1).astype(jnp.float32))
        adj_norm = (mask_blk.astype(jnp.float32) * scale_user[:, None] * scale_item[None, :]).astype(jnp.bfloat16)
        cur_user = user_shard
        cur_item = item_shard
        total_user = user_shard.astype(jnp.float32)
        total_item = item_shard.astype(jnp.float32)
        for layer_idx in range(LAYERS):
            item_panel = lax.all_gather(cur_item, "row", axis=0, tiled=True)
            user_panel = lax.all_gather(cur_user, "col", axis=0, tiled=True)
            user_part = jnp.dot(adj_norm, item_panel, preferred_element_type=jnp.float32)
            item_part = jnp.einsum("ui,ud->id", adj_norm, user_panel, preferred_element_type=jnp.float32)
            cur_user = lax.psum_scatter(user_part, "col", scatter_dimension=0, tiled=True).astype(jnp.bfloat16)
            cur_item = lax.psum_scatter(item_part, "row", scatter_dimension=0, tiled=True).astype(jnp.bfloat16)
            total_user = total_user + cur_user.astype(jnp.float32)
            total_item = total_item + cur_item.astype(jnp.float32)
        out_user = (total_user / (LAYERS + 1)).astype(jnp.bfloat16)
        out_item = (total_item / (LAYERS + 1)).astype(jnp.bfloat16)
        user_start = (row_idx * col_count + col_idx) * out_user.shape[0]
        item_start = (col_idx * row_count + row_idx) * out_item.shape[0]
        picked = jnp.concatenate([
            lookup(out_user, triples[:, 0], user_start),
            lookup(out_item, triples[:, 1], item_start),
            lookup(out_item, triples[:, 2], item_start),
        ], axis=0)
        picked = lax.psum(picked, ("row", "col"))
        batch_n = triples.shape[0]
        vec_user = picked[:batch_n]
        vec_pos = picked[batch_n:2 * batch_n]
        vec_neg = picked[2 * batch_n:]
        margin = jnp.sum(vec_user * vec_pos, axis=1) - jnp.sum(vec_user * vec_neg, axis=1)
        bpr_loss = jax.nn.softplus(-margin)
        return out_user, out_item, bpr_loss

    return jax.shard_map(
        device_body,
        mesh=mesh,
        in_specs=(P("row", "col"), P(("row", "col"), None), P(("col", "row"), None), P()),
        out_specs=(P(("row", "col"), None), P(("col", "row"), None), P()),
        check_vma=False,
    )
```

profile of v0, /device:TPU:1, one launch (start us, length us, event | category | flops | bytes accessed | tf_op | source)
XLA Modules:
  0.0 1046.5 jit_solution(3430394489142212444)
XLA Ops:
  7.2 0.0 reduce-scatter.6.cloned.1.call-start
  7.2 2.6 fusion.4
  9.8 20.8 %psum.22 = s32[1024]{0:T(1024)S(1)} all-reduce(s32[1024]{0:T(1024)S(1)} %get-tuple-element.5), channel_id=1, replica_groups=mesh['col'=4,'row'=64] {'row'}, use_global_device_ids=true, to_apply=%region_3.0 | all-reduce | flops 1024 | bytes 8192 | tf_op jit(solution)/shard_map/psum | solution.py:23
  30.6 7.2 psum.21
  37.8 9.1 all_gather.19
  46.9 2.7 multiply_convert_fusion
  49.6 0.0 copy-start.7
  49.6 0.7 fusion.6
  50.3 0.0 copy-start.6
  50.4 252.7 %all-reduce.9 = bf16[1024,64]{1,0:T(8,128)(2,1)S(1)} all-reduce(f32[1024,64]{1,0:T(8,128)S(1)} %fusion.6), channel_id=3, replica_groups=mesh['col'=4,'row'=64] {'row'}, use_global_device_ids=true, to_apply=%region_5.0.clone | all-reduce | flops 65536 | bytes 393216
  303.1 0.6 dynamic-slice
  304.3 52.4 %all_gather.20 = bf16[1024,64]{1,0:T(8,128)(2,1)S(1)} all-gather(bf16[16,64]{1,0:T(8,128)(2,1)S(1)} %dynamic-slice_convert_fusion.2), channel_id=1, replica_groups=mesh['col'=4,'row'=64] {'row'}, dimensions={0}, use_global_device_ids=true | all-gather | bytes 133120 | tf_op jit(solution)/shard_map/all_gather | solution.py:32
  356.7 1.5 fusion.7
  358.2 0.0 reduce-scatter.6.cloned.1.call-update
  358.2 0.0 reduce-scatter.4.cloned.1.call-start
  358.3 50.0 %all_gather.18 = bf16[1024,64]{1,0:T(8,128)(2,1)S(1)} all-gather(bf16[16,64]{1,0:T(8,128)(2,1)S(1)} %copy-done.6), channel_id=1, replica_groups=mesh['col'=4,'row'=64] {'row'}, dimensions={0}, use_global_device_ids=true | all-gather | bytes 133120 | tf_op jit(solution)/shard_map/all_gather | solution.py:32
  408.3 1.5 fusion.5
  409.8 0.0 reduce-scatter.4.cloned.1.call-update
  409.8 0.0 reduce-scatter.8.cloned.1.call-start
  409.9 0.1 and_reduce_fusion.2
  410.0 0.0 reduce-scatter.6.cloned.1.call-done
  410.0 0.8 convert_element_type.77
  410.9 9.5 all_gather.23
  420.4 0.7 fusion.10
  421.1 3.6 reduce-scatter.4.cloned.1.call-done
  424.8 0.8 convert_element_type.74
  425.6 9.1 all_gather.21
  434.7 0.7 fusion.8
  435.4 256.1 %all-reduce.10 = (bf16[1024,64]{1,0:T(8,128)(2,1)}, bf16[1024,64]{1,0:T(8,128)(2,1)}) all-reduce(f32[1024,64]{1,0:T(8,128)S(1)} %fusion.8, f32[1024,64]{1,0:T(8,128)S(1)} %fusion.10), channel_id=5, replica_groups=mesh['col'=4,'row'=64] {'row'}, use_global_device_ids=true, to_apply=%region_7.0.clone | all-reduce | flops 131072 | bytes 786432
  691.6 0.7 multiply_convert_fusion.2
  692.3 52.9 %all_gather.22 = bf16[1024,64]{1,0:T(8,128)(2,1)S(1)} all-gather(bf16[16,64]{1,0:T(8,128)(2,1)S(1)} %get-tuple-element.16), channel_id=1, replica_groups=mesh['col'=4,'row'=64] {'row'}, dimensions={0}, use_global_device_ids=true | all-gather | bytes 133120 | tf_op jit(solution)/shard_map/all_gather | solution.py:32
  745.2 1.5 fusion.9
  746.6 0.0 reduce-scatter.8.cloned.1.call-update
  746.6 0.0 all-reduce.8.cloned.1.call-start
  746.7 3.2 gather_fusion.1
  750.0 3.2 gather_fusion.2
  753.2 0.9 convert_select_fusion
  754.1 12.2 %reduce-scatter.8.cloned.1.call-done = f32[256,64]{0,1:T(8,128)} async-done(((f32[1024,64]{0,1:T(8,128)}), f32[256,64]{0,1:T(8,128)}) %reduce-scatter.8.cloned.1.call-update) | async-done | bytes 65552 | tf_op jit(solution)/shard_map/reduce_scatter | solution.py:36
  766.3 0.9 multiply_convert_fusion.1
  767.2 0.0 copy-start.4
  767.2 0.1 copy.8
  767.3 3.2 gather_fusion
  770.5 0.3 convert_select_fusion.2
  770.9 1.3 pad_maximum_fusion
  772.1 0.0 all-reduce.8.cloned.1.call-update
  772.2 265.5 %all-reduce.8.cloned.1.call-done = f32[3072,64]{1,0:T(8,128)} async-done(((f32[3072,64]{1,0:T(8,128)}), f32[3072,64]{1,0:T(8,128)}) %all-reduce.8.cloned.1.call-update) | async-done | bytes 786448 | tf_op jit(solution)/shard_map/psum | solution.py:49
  1037.6 1.7 fusion
  1039.3 0.6 compare_select_fusion.3
  (22 shorter events, 0.1 us)
Async XLA Ops:
  7.2 402.9 %reduce-scatter.6.cloned.1.call-start = ((), (), s32[]{:S(2)}) async-start(), calls=%async_computation.4 | async-start | bytes 327680 | tf_op jit(solution)/shard_map/reduce_scatter | solution.py:36
  7.2 30.5 %copy-start.3 = (bf16[256,64]{0,1:T(8,128)(2,1)S(1)}, bf16[256,64]{0,1:T(8,128)(2,1)}, u32[]{:S(2)}) copy-start(bf16[256,64]{0,1:T(8,128)(2,1)} %param.7) | copy-start | bytes 98308
  49.6 253.5 %copy-start.7 = (u32[256]{0:T(256)S(1)}, u32[256]{0:T(256)}, u32[]{:S(2)}) copy-start(u32[256]{0:T(256)} %constant.63) | copy-start | bytes 3076
  50.3 307.9 %copy-start.6 = (bf16[16,64]{1,0:T(8,128)(2,1)S(1)}, bf16[16,64]{1,0:T(8,128)(2,1)}, u32[]{:S(2)}) copy-start(bf16[16,64]{1,0:T(8,128)(2,1)} %param.8) | copy-start | bytes 6148
  358.2 51.7 %copy-start.5 = (s32[1024,3]{0,1:T(4,128)S(1)}, s32[1024,3]{0,1:T(4,128)}, u32[]{:S(2)}) copy-start(s32[1024,3]{0,1:T(4,128)} %param.9) | copy-start | bytes 36868
  358.2 66.6 %reduce-scatter.4.cloned.1.call-start = ((), (), s32[]{:S(2)}) async-start(), calls=%async_computation.3 | async-start | bytes 327680 | tf_op jit(solution)/shard_map/reduce_scatter | solution.py:36
  409.8 356.5 %reduce-scatter.8.cloned.1.call-start = ((), (), s32[]{:S(2)}) async-start(), calls=%async_computation.5 | async-start | bytes 327680 | tf_op jit(solution)/shard_map/reduce_scatter | solution.py:36
  692.3 57.7 %copy-start = (bf16[16,64]{1,0:T(8,128)(2,1)}, bf16[16,64]{1,0:T(8,128)(2,1)S(1)}, u32[]{:S(2)}) copy-start(bf16[16,64]{1,0:T(8,128)(2,1)S(1)} %get-tuple-element.15) | copy-start | bytes 6148
  746.6 291.0 %all-reduce.8.cloned.1.call-start = ((), (), s32[]{:S(2)}) async-start(), calls=%async_computation.6 | async-start | bytes 3145728 | tf_op jit(solution)/shard_map/psum | solution.py:49
  749.9 16.4 %copy-start.1 = (f32[256,64]{0,1:T(8,128)S(1)}, f32[256,64]{0,1:T(8,128)}, u32[]{:S(2)}) copy-start(f32[256,64]{0,1:T(8,128)} %reduce-scatter.6.cloned.1.call-done) | copy-start | bytes 196612
  750.0 16.4 %copy-start.2 = (f32[256,64]{0,1:T(8,128)S(1)}, f32[256,64]{0,1:T(8,128)}, u32[]{:S(2)}) copy-start(f32[256,64]{0,1:T(8,128)} %reduce-scatter.4.cloned.1.call-done) | copy-start | bytes 196612
  767.2 4.9 copy-start.4
Sparse Core Ops, SparseCore 0:
  358.3 16.2 reduce-scatter.5
  409.9 14.8 reduce-scatter.3
  746.8 19.5 reduce-scatter.7
  772.3 265.2 all-reduce.7
where the time goes:
time: 1050 us
  blocking collectives  720 us (69%)
  waiting for transfers between devices  281 us (27%)
  between operations  14.7 us (1%)
  other arithmetic  13.5 us (1%)
    unnamed x2, blocking collectives  509 us
    psum x1, waiting for transfers between devices, device_body(): picked = lax.psum(picked, ('row', 'col'))  265 us
    all_gather x3, blocking collectives, device_body(): item_panel = lax.all_gather(cur_item, 'row', axis=0, tiled=True)  155 us
    all_gather x3, blocking collectives, device_body(): user_panel = lax.all_gather(cur_user, 'col', axis=0, tiled=True)  27.7 us
  transfers between devices with their start and end apart: 4, of which 3 were waited for; matrix products, arithmetic and copies ran while one was open for 1% of the time, Pallas kernels for 0%

commit v1 on v0

v1 whole, which is shorter than its diff:
```python
import functools

import jax
import jax.numpy as jnp
from jax import lax
from jax.experimental import pallas as pl
from jax.experimental.pallas import tpu as pltpu
from jax.sharding import PartitionSpec as P

LAYERS = 3
LANES = 128
F32 = jnp.float32
BF16 = jnp.bfloat16
NT = (((1,), (1,)), ((), ()))
NN = (((1,), (0,)), ((), ()))

STAGES = (
    ("deg_user", "x"), ("deg_item_a", "yc"), ("deg_item_b", "z"),
    ("emb_user", "x"), ("emb_item_a", "yc"), ("emb_item_b", "z"),
    ("urs1", "x"), ("urs2", "x"), ("urs3", "x"),
    ("uag1", "x"), ("uag2", "x"), ("uag3", "x"),
    ("irs1", "yc"), ("irs2", "yc"), ("irs3", "yc"),
    ("izz1", "z"), ("izz2", "z"), ("izz3", "z"),
    ("iag1", "yc"), ("iag2", "yc"), ("iag3", "yc"),
    ("loss_x", "x"), ("loss_yc", "yc"), ("loss_z", "z"),
)
SID = {name: idx for idx, (name, _) in enumerate(STAGES)}
GROUP = dict(STAGES)
OFFSETS = {"x": (2, 1, 3), "yc": (4, 5, 3, 2, 6, 7, 1), "z": (4, 3, 5, 2, 6, 1, 7)}
SIZE = {"x": 4, "yc": 8, "z": 8}


def mm(lhs, rhs, dims):
    return lax.dot_general(lhs, rhs, dims, preferred_element_type=F32)


def eye(rows, cols):
    row_id = lax.broadcasted_iota(jnp.int32, (rows, cols), 0)
    col_id = lax.broadcasted_iota(jnp.int32, (rows, cols), 1)
    return jnp.where(row_id == col_id, 1.0, 0.0).astype(BF16)


def kernel(axis_names, mask_hbm, user_ref, item_ref, trip_ref,
           out_user_ref, out_item_ref, loss_ref,
           mask_v, mask_b, adj, hot_user, hot_item, row_part, su_col, si_row, row_t,
           small_src, item_tr, user_src, part_user, own_user, part_item, own_item, marg,
           deg_user_s, deg_item_a, deg_item_b, emb_user_s, emb_item_a, emb_item_b,
           urs1, urs2, urs3, uag1, uag2, uag3,
           irs1, irs2, irs3, izz1, izz2, izz3, iag1, iag2, iag3,
           loss_x, loss_yc, loss_z,
           load_sem, send_sem, recv_sem):
    slots = {"deg_user": deg_user_s, "deg_item_a": deg_item_a, "deg_item_b": deg_item_b,
             "emb_user": emb_user_s, "emb_item_a": emb_item_a, "emb_item_b": emb_item_b,
             "urs1": urs1, "urs2": urs2, "urs3": urs3, "uag1": uag1, "uag2": uag2, "uag3": uag3,
             "irs1": irs1, "irs2": irs2, "irs3": irs3, "izz1": izz1, "izz2": izz2, "izz3": izz3,
             "iag1": iag1, "iag2": iag2, "iag3": iag3,
             "loss_x": loss_x, "loss_yc": loss_yc, "loss_z": loss_z}
    row = lax.axis_index("row")
    col = lax.axis_index("col")
    zed = row // 8
    pos = row % 8
    here = {"x": col, "yc": pos, "z": zed}

    def device(group, idx):
        coord = {"col": col, "row": row}
        if group == "x":
            coord["col"] = idx
        elif group == "yc":
            coord["row"] = zed * 8 + idx
        else:
            coord["row"] = idx * 8 + pos
        return tuple(coord[name] for name in axis_names)

    def peers(group):
        return [(here[group] + off) % SIZE[group] for off in OFFSETS[group]]

    def send(name, src, idx):
        group = GROUP[name]
        pltpu.make_async_remote_copy(
            src_ref=src, dst_ref=slots[name].at[here[group]],
            send_sem=send_sem.at[SID[name]], recv_sem=recv_sem.at[SID[name]],
            device_id=device(group, idx), device_id_type=pl.DeviceIdType.MESH).start()

    def send_all(name, src):
        for idx in peers(GROUP[name]):
            send(name, src, idx)

    def whole(name):
        group = GROUP[name]
        part = slots[name].at[pl.ds(0, SIZE[group] - 1)]
        return pltpu.make_async_remote_copy(
            src_ref=part, dst_ref=part,
            send_sem=send_sem.at[SID[name]], recv_sem=recv_sem.at[SID[name]],
            device_id=device(group, (here[group] + 1) % SIZE[group]),
            device_id_type=pl.DeviceIdType.MESH)

    def arrive(name):
        whole(name).wait_recv()

    def total(name):
        buf = slots[name]
        acc = buf[0]
        for idx in range(1, SIZE[GROUP[name]]):
            acc = acc + buf[idx]
        return acc

    def panel(name):
        buf = slots[name]
        return jnp.concatenate([buf[idx] for idx in range(SIZE[GROUP[name]])], axis=1)

    barrier = pltpu.get_barrier_semaphore()
    n_peers = 0
    for group in ("z", "yc", "x"):
        for idx in peers(group):
            pl.semaphore_signal(barrier, inc=1, device_id=device(group, idx),
                                device_id_type=pl.DeviceIdType.MESH)
            n_peers += 1
    loads = []
    for q in range(4):
        cp = pltpu.make_async_copy(mask_hbm.at[pl.ds(q * 256, 256)], mask_v.at[pl.ds(q * 256, 256)], load_sem.at[q])
        cp.start()
        loads.append(cp)
    eye64 = eye(64, 64)
    user_t = mm(eye64, user_ref[...], NT).astype(BF16)
    user_src[0] = user_t
    emb_user_s[col] = user_t
    emb_item_a[pos] = item_ref[...]
    pl.semaphore_wait(barrier, n_peers)
    send_all("emb_item_a", item_ref)
    send_all("emb_user", user_src.at[0])

    def degree_rows(blk, acc):
        base = pl.multiple_of(blk * 32, 32)
        m = mask_v[pl.ds(base, 32), :].astype(F32)
        mask_b[pl.ds(base, 32), :] = m.astype(BF16)
        part = m[:, 0:LANES]
        for k in range(1, 8):
            part = part + m[:, k * LANES:(k + 1) * LANES]
        row_part[pl.ds(base, 32), :] = part.astype(BF16)
        return acc + ((m[0:8] + m[8:16]) + (m[16:24] + m[24:32]))

    acc = jnp.zeros((8, 1024), F32)
    for q in range(4):
        loads[q].wait()
        acc = lax.fori_loop(q * 8, (q + 1) * 8, degree_rows, acc)
    col_sum = jnp.sum(acc, axis=0, keepdims=True)
    for k in range(8):
        small_src[0, k:k + 1, :] = col_sum[:, k * LANES:(k + 1) * LANES]
    deg_item_a[pos] = small_src[0]
    send_all("deg_item_a", small_src.at[0])
    row_sum = mm(jnp.ones((8, LANES), BF16), row_part[...], NT)
    for k in range(8):
        small_src[1, k:k + 1, :] = row_sum[0:1, k * LANES:(k + 1) * LANES]
    deg_user_s[col] = small_src[1]
    send_all("deg_user", small_src.at[1])

    def one_hot(blk, carry):
        base = pl.multiple_of(blk * 16, 16)
        trip = trip_ref[pl.ds(base, 16), :]
        lane = lax.broadcasted_iota(jnp.int32, (16, 1024), 1)
        hit = lambda ids: jnp.where(ids == lane, 1.0, 0.0)
        hot_user[pl.ds(base, 16), :] = hit(trip[:, 0:1] - row * 1024).astype(BF16)
        hot_item[pl.ds(base, 16), :] = (hit(trip[:, 1:2] - col * 1024) - hit(trip[:, 2:3] - col * 1024)).astype(BF16)
        return carry

    arrive("emb_item_a")
    gathered = jnp.concatenate([emb_item_a[k] for k in range(8)], axis=0)
    item_t = mm(eye64, gathered, NT).astype(BF16)
    item_tr[...] = item_t
    emb_item_b[zed] = item_t
    send_all("emb_item_b", item_tr)
    lax.fori_loop(0, 32, one_hot, 0)
    arrive("deg_item_a")
    deg_sum = total("deg_item_a")
    small_src[2] = deg_sum
    deg_item_b[zed] = deg_sum
    send_all("deg_item_b", small_src.at[2])
    lax.fori_loop(32, 64, one_hot, 0)
    arrive("deg_user")
    scale_user = lax.rsqrt(jnp.maximum(total("deg_user"), 1.0))
    for k in range(8):
        su_col[pl.ds(k * LANES, LANES), :] = jnp.transpose(jnp.broadcast_to(scale_user[k:k + 1, :], (LANES, LANES)))
    arrive("emb_user")
    arrive("emb_item_b")
    arrive("deg_item_b")
    scale_item = lax.rsqrt(jnp.maximum(total("deg_item_b"), 1.0))
    for k in range(8):
        si_row[:, k * LANES:(k + 1) * LANES] = jnp.broadcast_to(scale_item[k:k + 1, :], (8, LANES))

    def build(blk, carry):
        base = pl.multiple_of(blk * 16, 16)
        m = mask_b[pl.ds(base, 16), :].astype(F32)
        su = su_col[pl.ds(base, 16), :]
        for k in range(8):
            si = si_row[0:8, k * LANES:(k + 1) * LANES]
            si2 = jnp.concatenate([si, si], axis=0)
            adj[pl.ds(base, 16), k * LANES:(k + 1) * LANES] = ((m[:, k * LANES:(k + 1) * LANES] * su) * si2).astype(BF16)
        return carry

    lax.fori_loop(0, 64, build, 0)

    yy = pos // 2

    def item_products(layer, user_panel):
        name = f"irs{layer}"
        buf = part_item.at[layer - 1]
        for off in (2, 1, 3, 0):
            other = (yy + off) % 4
            cols = pl.ds(pl.multiple_of(other * 256, 256), 256)
            res = mm(user_panel, adj[:, cols], NN)
            buf[other * 2] = res[:, 0:LANES]
            buf[other * 2 + 1] = res[:, LANES:2 * LANES]
            if off:
                send(name, buf.at[other * 2], other * 2)
                send(name, buf.at[other * 2 + 1], other * 2 + 1)
            else:
                mate = other * 2 + (pos + 1) % 2
                send(name, buf.at[mate], mate)
        slots[name][pos] = buf[pos]

    def user_products(layer, item_panel):
        name = f"urs{layer}"
        buf = part_user.at[layer - 1]
        for off in (2, 1, 3, 0):
            other = (col + off) % 4
            rows = pl.ds(pl.multiple_of(other * 256, 256), 256)
            res = mm(item_panel, adj[rows, :], NT)
            if off:
                buf[other] = res
                send(name, buf.at[other], other)
            else:
                slots[name][col] = res

    def item_mid(layer):
        arrive(f"irs{layer}")
        val = total(f"irs{layer}")
        own_item[layer - 1] = val
        slots[f"izz{layer}"][zed] = val
        send_all(f"izz{layer}", own_item.at[layer - 1])

    tot_user = user_t.astype(F32)
    tot_item = emb_item_b[pos].astype(F32)

    def user_end(layer, tot):
        arrive(f"urs{layer}")
        val = total(f"urs{layer}").astype(BF16)
        tot = tot + val.astype(F32)
        res = val if layer < LAYERS else (tot * 0.25).astype(BF16)
        user_src[layer] = res
        slots[f"uag{layer}"][col] = res
        send_all(f"uag{layer}", user_src.at[layer])
        return tot

    def item_end(layer, tot):
        arrive(f"izz{layer}")
        val = total(f"izz{layer}").astype(BF16)
        tot = tot + val.astype(F32)
        res = val if layer < LAYERS else (tot * 0.25).astype(BF16)
        row_t[layer - 1] = res
        slots[f"iag{layer}"][pos] = res
        send_all(f"iag{layer}", row_t.at[layer - 1])
        return tot

    item_products(1, panel("emb_user"))
    user_products(1, panel("emb_item_b"))
    for layer in (1, 2):
        item_mid(layer)
        tot_user = user_end(layer, tot_user)
        arrive(f"uag{layer}")
        item_products(layer + 1, panel(f"uag{layer}"))
        tot_item = item_end(layer, tot_item)
        arrive(f"iag{layer}")
        user_products(layer + 1, panel(f"iag{layer}"))
    item_mid(3)
    user_end(3, tot_user)
    out_user_ref[...] = mm(eye(256, 256), user_src[3], NT).astype(BF16)
    arrive("uag3")
    picked_user = mm(panel("uag3"), hot_user[...], NT)
    item_end(3, tot_item)
    arrive("iag3")
    picked_item = mm(panel("iag3"), hot_item[...], NT)
    prod = picked_user * picked_item
    red = jnp.sum(prod, axis=0, keepdims=True)
    for k in range(8):
        marg[0, k:k + 1, :] = red[:, k * LANES:(k + 1) * LANES]
    loss_x[col] = marg[0]
    send_all("loss_x", marg.at[0])
    row_id = lax.broadcasted_iota(jnp.int32, (16, LANES), 0) + pos * 16
    col_id = lax.broadcasted_iota(jnp.int32, (16, LANES), 1)
    pick = jnp.where(row_id == col_id, 1.0, 0.0).astype(BF16)
    out_item_ref[...] = mm(pick, iag3[zed], NT).astype(BF16)
    arrive("loss_x")
    val = total("loss_x")
    marg[1] = val
    loss_yc[pos] = val
    send_all("loss_yc", marg.at[1])
    arrive("loss_yc")
    val = total("loss_yc")
    marg[2] = val
    loss_z[zed] = val
    send_all("loss_z", marg.at[2])
    arrive("loss_z")
    neg = -total("loss_z")
    loss_ref[...] = jnp.maximum(neg, 0.0) + jnp.log1p(jnp.exp(-jnp.abs(neg)))
    for name, _ in STAGES:
        whole(name).wait_send()


def solution(mesh):
    vm = pltpu.VMEM
    shapes = {
        "deg_user": ((4, 8, 128), F32), "deg_item_a": ((8, 8, 128), F32), "deg_item_b": ((8, 8, 128), F32),
        "emb_user": ((4, 64, 256), BF16), "emb_item_a": ((8, 16, 64), BF16), "emb_item_b": ((8, 64, 128), BF16),
    }
    for layer in (1, 2, 3):
        shapes[f"urs{layer}"] = ((4, 64, 256), F32)
        shapes[f"uag{layer}"] = ((4, 64, 256), BF16)
        shapes[f"irs{layer}"] = ((8, 64, 128), F32)
        shapes[f"izz{layer}"] = ((8, 64, 128), F32)
        shapes[f"iag{layer}"] = ((8, 64, 128), BF16)
    shapes["loss_x"] = ((4, 8, 128), F32)
    shapes["loss_yc"] = ((8, 8, 128), F32)
    shapes["loss_z"] = ((8, 8, 128), F32)
    scratch = [
        vm((1024, 1024), jnp.int32), vm((1024, 1024), BF16), vm((1024, 1024), BF16),
        vm((1024, 1024), BF16), vm((1024, 1024), BF16), vm((1024, 128), BF16),
        vm((1024, 128), F32), vm((8, 1024), F32), vm((3, 64, 128), BF16),
        vm((3, 8, 128), F32), vm((64, 128), BF16), vm((4, 64, 256), BF16),
        vm((3, 4, 64, 256), F32), vm((8, 128), F32), vm((3, 8, 64, 128), F32),
        vm((3, 64, 128), F32), vm((3, 8, 128), F32),
    ]
    scratch += [vm(*shapes[name]) for name, _ in STAGES]
    scratch += [pltpu.SemaphoreType.DMA((4,)), pltpu.SemaphoreType.DMA((len(STAGES),)),
                pltpu.SemaphoreType.DMA((len(STAGES),))]
    in_vmem = pl.BlockSpec(memory_space=pltpu.VMEM)
    call = pl.pallas_call(
        functools.partial(kernel, tuple(mesh.axis_names)),
        out_shape=(jax.ShapeDtypeStruct((256, 64), BF16), jax.ShapeDtypeStruct((16, 64), BF16),
                   jax.ShapeDtypeStruct((8, 128), F32)),
        in_specs=[pl.BlockSpec(memory_space=pl.ANY), in_vmem, in_vmem, in_vmem],
        out_specs=(in_vmem, in_vmem, in_vmem),
        scratch_shapes=scratch,
        compiler_params=pltpu.CompilerParams(collective_id=0, has_side_effects=True),
    )

    def device_body(mask_blk, user_shard, item_shard, triples):
        out_user, out_item, loss = call(mask_blk, user_shard, item_shard, triples)
        return out_user, out_item, loss.reshape(-1)

    return jax.shard_map(
        device_body,
        mesh=mesh,
        in_specs=(P("row", "col"), P(("row", "col"), None), P(("col", "row"), None), P()),
        out_specs=(P(("row", "col"), None), P(("col", "row"), None), P()),
        check_vma=False,
    )
```

time: 1050 us -> 90.5 us (0.09)
  blocking collectives: 720 us -> 0 us
  waiting for transfers between devices: 281 us -> 0 us
  Pallas kernels: 0 us -> 82.2 us
  between operations: 14.7 us -> 0.64 us
  other arithmetic: 13.5 us -> 0 us
    unnamed x2 -> x0, blocking collectives: 509 us -> none
    psum x1 -> x0, waiting for transfers between devices: 265 us -> none  [device_body(): picked = lax.psum(picked, ('row', 'col'))]
    all_gather x6 -> x0, blocking collectives: 183 us -> none  [the longest x3 155 us: device_body(): item_panel = lax.all_gather(cur_item, 'row', axis=0, tiled=True)]
    pallas_call x0 -> x1, Pallas kernels: none -> 82.2 us  [device_body(): out_user, out_item, loss = call(mask_blk, user_shard, item_shard, triples)]
    psum x2 -> x0, blocking collectives: 27.9 us -> none  [the longest x1 20.8 us: device_body(): deg_item = lax.psum(jnp.sum(mask_blk, axis=0), 'row')]
    reduce_scatter x3 -> x0, waiting for transfers between devices: 15.9 us -> none  [device_body(): lax.psum_scatter(user_part, 'col', scatter_dimension=0, tiled=True)]
  transfers between devices with their start and end apart: 4 -> 0, of which waited for: 3 -> 0; matrix products, arithmetic and copies ran while one was open for 1% -> 0% of each run, Pallas kernels for 0% -> 0%
where the time goes in v1:
time: 90.5 us; the launch traced here: 90.1 us
  Pallas kernels  82.2 us (91%)
  local copies, waits for them, and re-layouts  7.31 us (8%)
    pallas_call x1, Pallas kernels, device_body(): out_user, out_item, loss = call(mask_blk, user_shard, item_shard, triples)  82.2 us
    unnamed x5, local copies, waits for them, and re-layouts  7.31 us

profile of v1, /device:TPU:1, one launch (start us, length us, event | category | flops | bytes accessed | tf_op | source)
XLA Modules:
  0.0 90.1 jit_solution(4101411571247277156)
XLA Ops:
  0.6 1.5 %copy.7.user_ref = bf16[256,64]{1,0:T(8,128)(2,1)} copy(bf16[256,64]{0,1:T(8,128)(2,1)} %param.5) | data formatting | bytes 65536 | tf_op args[1]
  2.1 1.7 %copy.8.trip_ref = s32[1024,3]{1,0:T(8,128)} copy(s32[1024,3]{0,1:T(4,128)} %param.7) | data formatting | bytes 24576 | tf_op args[3]
  3.9 82.2 %shard_map.67 = (bf16[256,64]{1,0:T(8,128)(2,1)}, bf16[16,64]{1,0:T(8,128)(2,1)}, f32[8,128]{1,0:T(8,128)}) custom-call(s32[1024,1024]{1,0:T(8,128)} %mask_hbm.1, bf16[256,64]{1,0:T(8,128)(2,1)} %copy.7.user_ref, bf16[16,64]{1,0:T(8,128)(2,1)} %item_ref.1, s32[1024,3]{1,0:T(8,128)} %copy.8.trip_ref), custom_call_target="tpu_custom_call" | custom-call | tf_op jit(solution)/shard_map/pallas_call | solution.py:347
  86.1 1.5 %copy.9 = bf16[256,64]{0,1:T(8,128)(2,1)} copy(bf16[256,64]{1,0:T(8,128)(2,1)} %get-tuple-element.9) | data formatting | bytes 65536
  87.6 1.3 %copy.12 = bf16[16,64]{1,0:T(8,128)(2,1)} copy(bf16[16,64]{1,0:T(8,128)(2,1)} %get-tuple-element.16) | data formatting | bytes 4096
  88.9 1.3 %copy.13 = f32[1024]{0:T(1024)} copy(f32[1024]{0:T(1024)} %bitcast.1) | data formatting | bytes 8192

commit v2 on v0

v2 whole, which is shorter than its diff:
```python
import functools

import jax
import jax.numpy as jnp
from jax import lax
from jax.experimental import pallas as pl
from jax.experimental.pallas import tpu as pltpu
from jax.sharding import PartitionSpec as P

LAYERS = 3
LANES = 128
F32 = jnp.float32
BF16 = jnp.bfloat16
I32 = jnp.int32
NT = (((1,), (1,)), ((), ()))
NN = (((1,), (0,)), ((), ()))

YC = (4, 5, 3, 2, 6, 7, 1)
X, Y, Z, YP, XYC = range(5)
SIZE = (4, 8, 8, 16, 32)
OFFSETS = (
    (2, 1, 3),
    YC,
    (4, 3, 5, 2, 6, 1, 7),
    tuple(8 + off for off in YC + (0,)) + YC,
    tuple(8 * dx + off for dx in (2, 1, 3, 0) for off in YC + (0,) if dx or off),
)
(DEG_USER, DEG_ITEM_A, DEG_ITEM_B, EMB_USER, EMB_ITEM_A, EMB_ITEM_B, LOSS_A, LOSS_Z) = range(8)
URS, UAG, IRS, IZZ, IAG = 7, 10, 13, 16, 19
STAGES = (
    (X, (8, 128), F32), (Y, (8, 128), F32), (Z, (8, 128), F32),
    (X, (64, 256), BF16), (Y, (16, 64), BF16), (Z, (64, 128), BF16),
    (XYC, (8, 128), F32), (Z, (8, 128), F32),
    *[(X, (64, 256), F32)] * 3, *[(X, (64, 256), BF16)] * 3,
    *[(Y, (64, 128), F32)] * 3, *[(Z, (32, 128), F32)] * 3, *[(YP, (32, 128), BF16)] * 3,
)
SCRATCH = (
    ((1024, 1024), I32), ((1024, 1024), BF16), ((1024, 1024), BF16),
    ((1024, 1024), BF16), ((1024, 1024), BF16), ((1024, 128), BF16),
    ((1024, 128), F32), ((8, 1024), F32), ((3, 8, 1024), I32),
    ((5, 8, 128), F32), ((64, 128), BF16), ((3, 64, 256), BF16),
    ((3, 4, 64, 256), F32), ((3, 8, 64, 128), F32),
    ((3, 64, 128), F32), ((3, 32, 128), BF16),
    ((64, 256), BF16), ((16, 64), BF16), ((3, 1024), I32),
)


class Stop(Exception):
    pass


def mm(lhs, rhs, dims):
    return lax.dot_general(lhs, rhs, dims, preferred_element_type=F32)


def eye(rows, cols):
    row_id = lax.broadcasted_iota(I32, (rows, cols), 0)
    col_id = lax.broadcasted_iota(I32, (rows, cols), 1)
    return jnp.where(row_id == col_id, 1.0, 0.0).astype(BF16)


def kernel(axis_names, stop, mask_hbm, user_hbm, item_hbm, trip_hbm, out_user_ref, out_item_ref, loss_ref, *refs):
    (mask_v, mask_b, adj, hot_user, hot_item, row_part, su_col, si_row, ids, small, item_tr, user_src,
     part_user, part_item, own_item, out_half, user_ref, item_ref, trip_ref) = refs[:len(SCRATCH)]
    slots = refs[len(SCRATCH):-3]
    load_sem, send_sem, recv_sem = refs[-3:]
    row = lax.axis_index("row")
    col = lax.axis_index("col")
    zed = row // 8
    pos = row % 8
    par = zed % 2
    here = (col, pos, zed, par * 8 + pos, col * 8 + pos)
    started, arrived, loads = [], [], []

    def device(group, idx):
        to_col, to_row = col, row
        if group == X:
            to_col = idx
        elif group == Y:
            to_row = zed * 8 + idx
        elif group == Z:
            to_row = idx * 8 + pos
        elif group == YP:
            to_row = (zed - par + idx // 8) * 8 + idx % 8
        else:
            to_col = idx // 8
            to_row = zed * 8 + idx % 8
        return tuple(to_col if name == "col" else to_row for name in axis_names)

    def peers(group):
        if group == YP:
            return [(par + off // 8) % 2 * 8 + (pos + off % 8) % 8 for off in OFFSETS[group]]
        if group == XYC:
            return [(col + off // 8) % 4 * 8 + (pos + off % 8) % 8 for off in OFFSETS[group]]
        return [(here[group] + off) % SIZE[group] for off in OFFSETS[group]]

    def send(stage, src, idx):
        if stage not in started:
            started.append(stage)
        group = STAGES[stage][0]
        pltpu.make_async_remote_copy(
            src_ref=src, dst_ref=slots[stage].at[here[group]],
            send_sem=send_sem.at[stage], recv_sem=recv_sem.at[stage],
            device_id=device(group, idx), device_id_type=pl.DeviceIdType.MESH).start()

    def send_all(stage, src):
        for idx in peers(STAGES[stage][0]):
            send(stage, src, idx)

    def whole(stage):
        group = STAGES[stage][0]
        part = slots[stage].at[pl.ds(0, SIZE[group] - 1)]
        return pltpu.make_async_remote_copy(
            src_ref=part, dst_ref=part, send_sem=send_sem.at[stage], recv_sem=recv_sem.at[stage],
            device_id=device(group, peers(group)[0]), device_id_type=pl.DeviceIdType.MESH)

    def arrive(stage):
        arrived.append(stage)
        whole(stage).wait_recv()

    def total(stage):
        buf = slots[stage]
        acc = buf[0]
        for idx in range(1, SIZE[STAGES[stage][0]]):
            acc = acc + buf[idx]
        return acc

    def panel(stage):
        buf = slots[stage]
        group = STAGES[stage][0]
        if group == YP:
            halves = [jnp.concatenate([buf[8 * k + idx] for idx in range(8)], axis=1) for k in (0, 1)]
            return jnp.concatenate(halves, axis=0)
        return jnp.concatenate([buf[idx] for idx in range(SIZE[group])], axis=1)

    def mark(point):
        if stop == point:
            raise Stop

    def lanes(k):
        return slice(k * LANES, (k + 1) * LANES)

    def load(src, dst):
        cp = pltpu.make_async_copy(src, dst, load_sem.at[len(loads)])
        cp.start()
        loads.append(cp)
        return cp

    def body():
        barrier = pltpu.get_barrier_semaphore()
        n_peers = 0
        for group in (Z, XYC, YP):
            for off, idx in zip(OFFSETS[group], peers(group), strict=True):
                if group != YP or off >= 8:
                    pl.semaphore_signal(barrier, inc=1, device_id=device(group, idx),
                                        device_id_type=pl.DeviceIdType.MESH)
                    n_peers += 1
        for q in range(4):
            rows = pl.ds(q * 256, 256)
            load(mask_hbm.at[rows], mask_v.at[rows])
        user_cp = load(user_hbm, user_ref)
        item_cp = load(item_hbm, item_ref)
        trip_cp = load(trip_hbm, trip_ref)

        if stop == 0:
            pl.semaphore_wait(barrier, n_peers)
            for cp in loads:
                cp.wait()
            raise Stop

        def degree_rows(blk, acc):
            base = pl.multiple_of(blk * 32, 32)
            m = mask_v[pl.ds(base, 32), :].astype(F32)
            mask_b[pl.ds(base, 32), :] = m.astype(BF16)
            part = m[:, lanes(0)]
            for k in range(1, 8):
                part = part + m[:, lanes(k)]
            row_part[pl.ds(base, 32), :] = part.astype(BF16)
            return acc + ((m[0:8] + m[8:16]) + (m[16:24] + m[24:32]))

        acc = jnp.zeros((8, 1024), F32)
        for q in range(4):
            loads[q].wait()
            acc = lax.fori_loop(q * 8, (q + 1) * 8, degree_rows, acc)
        col_sum = jnp.sum(acc, axis=0, keepdims=True)
        for k in range(8):
            small[0, k:k + 1, :] = col_sum[:, lanes(k)]
        slots[DEG_ITEM_A][pos] = small[0]
        row_sum = mm(jnp.ones((8, LANES), BF16), row_part[...], NT)
        for k in range(8):
            small[1, k:k + 1, :] = row_sum[0:1, lanes(k)]
        slots[DEG_USER][col] = small[1]
        for cp in (user_cp, item_cp, trip_cp):
            cp.wait()
        pl.semaphore_wait(barrier, n_peers)
        mark(1)
        send_all(DEG_ITEM_A, small.at[0])
        send_all(DEG_USER, small.at[1])
        mark(2)
        send_all(EMB_USER, user_ref)
        send_all(EMB_ITEM_A, item_ref)
        user_t = user_ref[...]
        slots[EMB_USER][col] = user_t
        slots[EMB_ITEM_A][pos] = item_ref[...]
        ids[0] = jnp.broadcast_to(trip_ref[0:1, :] - row * 1024, (8, 1024))
        ids[1] = jnp.broadcast_to(trip_ref[1:2, :] - col * 1024, (8, 1024))
        ids[2] = jnp.broadcast_to(trip_ref[2:3, :] - col * 1024, (8, 1024))

        def one_hot(blk, carry):
            base = pl.multiple_of(blk * 16, 16)
            for k in range(8):
                hits = []
                for half in range(2):
                    sub = lax.broadcasted_iota(I32, (8, LANES), 0) + (base + half * 8)
                    hits.append([jnp.where(ids[w, :, lanes(k)] == sub, 1.0, 0.0) for w in range(3)])
                hot_user[pl.ds(base, 16), lanes(k)] = jnp.concatenate([hit[0] for hit in hits], axis=0).astype(BF16)
                hot_item[pl.ds(base, 16), lanes(k)] = jnp.concatenate([hit[1] - hit[2] for hit in hits], axis=0).astype(BF16)
            return carry

        def item_columns(stage, layer, user_panel, prepare=None):
            buf = part_item.at[layer - 1]
            for off in (2, 1, 3, 0):
                other = (pos // 2 + off) % 4
                cols = pl.ds(pl.multiple_of(other * 256, 256), 256)
                if prepare is not None:
                    prepare(cols)
                res = mm(user_panel, adj[:, cols], NN)
                buf[other * 2] = res[:, lanes(0)]
                buf[other * 2 + 1] = res[:, lanes(1)]
                if off:
                    send(stage, buf.at[other * 2], other * 2)
                    send(stage, buf.at[other * 2 + 1], other * 2 + 1)
                else:
                    mate = other * 2 + (pos + 1) % 2
                    send(stage, buf.at[mate], mate)
            slots[stage][pos] = buf[pos]

        arrive(DEG_ITEM_A)
        deg_sum = total(DEG_ITEM_A)
        small[2] = deg_sum
        slots[DEG_ITEM_B][zed] = deg_sum
        send_all(DEG_ITEM_B, small.at[2])
        mark(3)
        arrive(EMB_ITEM_A)
        gathered = jnp.concatenate([slots[EMB_ITEM_A][k] for k in range(8)], axis=0)
        item_t = mm(eye(64, 64), gathered, NT).astype(BF16)
        item_tr[...] = item_t
        slots[EMB_ITEM_B][zed] = item_t
        send_all(EMB_ITEM_B, item_tr)
        arrive(DEG_USER)
        scale_user = lax.rsqrt(jnp.maximum(total(DEG_USER), 1.0))
        for k in range(8):
            su_col[pl.ds(k * LANES, LANES), :] = jnp.transpose(jnp.broadcast_to(scale_user[k:k + 1, :], (LANES, LANES)))
        lax.fori_loop(0, 64, one_hot, 0)
        arrive(EMB_USER)
        mark(4)
        arrive(DEG_ITEM_B)
        scale_item = lax.rsqrt(jnp.maximum(total(DEG_ITEM_B), 1.0))
        for k in range(8):
            si_row[:, lanes(k)] = jnp.broadcast_to(scale_item[k:k + 1, :], (8, LANES))

        def prepare(cols):
            si = si_row[:, cols]

            def build(blk, carry):
                base = pl.multiple_of(blk * 16, 16)
                su = su_col[pl.ds(base, 16), :]
                m = mask_b[pl.ds(base, 16), cols].astype(F32)
                for k in range(2):
                    si2 = jnp.concatenate([si[:, lanes(k)]] * 2, axis=0)
                    val = ((m[:, lanes(k)] * su) * si2).astype(BF16)
                    adj[pl.ds(base, 16), pl.ds(pl.multiple_of(cols.start + k * LANES, LANES), LANES)] = val
                return carry

            lax.fori_loop(0, 64, build, 0)

        def user_products(layer, item_panel):
            buf = part_user.at[layer - 1]
            for off in (2, 1, 3, 0):
                other = (col + off) % 4
                rows = pl.ds(pl.multiple_of(other * 256, 256), 256)
                res = mm(item_panel, adj[rows, :], NT)
                if off:
                    buf[other] = res
                    send(URS + layer, buf.at[other], other)
                else:
                    slots[URS + layer][col] = res

        def item_mid(layer):
            own = own_item.at[layer - 1]
            arrive(IRS + layer)
            own[...] = total(IRS + layer)
            for idx in peers(Z):
                send(IZZ + layer, own.at[pl.ds(pl.multiple_of(idx % 2 * 32, 32), 32)], idx)
            slots[IZZ + layer][zed] = own[pl.ds(pl.multiple_of(par * 32, 32), 32)]

        def finish(stage, to, keep, layer, tot, place):
            arrive(stage)
            val = total(stage).astype(BF16)
            tot = tot + val.astype(F32)
            res = val if layer < LAYERS else (tot * 0.25).astype(BF16)
            keep[layer - 1] = res
            slots[to][place] = res
            send_all(to, keep.at[layer - 1])
            return tot

        def user_end(layer, tot):
            return finish(URS + layer, UAG + layer, user_src, layer, tot, col)

        def item_end(layer, tot):
            return finish(IZZ + layer, IAG + layer, out_half, layer, tot, par * 8 + pos)

        tot_user = user_t.astype(F32)
        item_columns(IRS + 1, 1, panel(EMB_USER), prepare)
        mark(5)
        arrive(EMB_ITEM_B)
        tot_item = slots[EMB_ITEM_B][pos, pl.ds(pl.multiple_of(par * 32, 32), 32)].astype(F32)
        user_products(1, panel(EMB_ITEM_B))
        mark(6)
        item_mid(1)
        mark(7)
        tot_user = user_end(1, tot_user)
        arrive(UAG + 1)
        item_columns(IRS + 2, 2, panel(UAG + 1))
        mark(8)
        tot_item = item_end(1, tot_item)
        mark(9)
        item_mid(2)
        arrive(IAG + 1)
        user_products(2, panel(IAG + 1))
        mark(10)
        tot_item = item_end(2, tot_item)
        tot_user = user_end(2, tot_user)
        mark(11)
        arrive(UAG + 2)
        item_columns(IRS + 3, 3, panel(UAG + 2))
        mark(12)
        arrive(IAG + 2)
        user_products(3, panel(IAG + 2))
        item_mid(3)
        mark(13)
        user_end(3, tot_user)
        out_user_ref[...] = user_src[2]
        arrive(UAG + 3)
        picked_user = mm(panel(UAG + 3), hot_user[...], NN)
        item_end(3, tot_item)
        mark(14)
        arrive(IAG + 3)
        picked_item = mm(panel(IAG + 3), hot_item[...], NN)
        red = jnp.sum(picked_user * picked_item, axis=0, keepdims=True)
        for k in range(8):
            small[3, k:k + 1, :] = red[:, lanes(k)]
        slots[LOSS_A][col * 8 + pos] = small[3]
        send_all(LOSS_A, small.at[3])
        mark(15)
        row_id = lax.broadcasted_iota(I32, (16, LANES), 0) + pos * 16
        col_id = lax.broadcasted_iota(I32, (16, LANES), 1)
        pick = jnp.where(row_id == col_id, 1.0, 0.0).astype(BF16)
        block = jnp.concatenate([slots[IAG + 3][zed], slots[IAG + 3][8 + zed]], axis=0)
        out_item_ref[...] = mm(pick, block, NT).astype(BF16)
        arrive(LOSS_A)
        val = total(LOSS_A)
        small[4] = val
        slots[LOSS_Z][zed] = val
        send_all(LOSS_Z, small.at[4])
        arrive(LOSS_Z)
        neg = -total(LOSS_Z)
        loss_ref[...] = jnp.maximum(neg, 0.0) + jnp.log1p(jnp.exp(-jnp.abs(neg)))

    try:
        body()
    except Stop:
        pass
    for stage in started:
        if stage not in arrived:
            arrive(stage)
        whole(stage).wait_send()


def hand_over(user_in, item_in, loss_in, user_out, item_out, loss_out):
    user_out[...] = user_in[...]
    item_out[...] = item_in[...]
    loss_out[...] = loss_in[...]


def solution(mesh, stop=None):
    scratch = [pltpu.VMEM(*spec) for spec in SCRATCH]
    scratch += [pltpu.VMEM((SIZE[group],) + shape, dtype) for group, shape, dtype in STAGES]
    scratch += [pltpu.SemaphoreType.DMA((7,)), pltpu.SemaphoreType.DMA((len(STAGES),)),
                pltpu.SemaphoreType.DMA((len(STAGES),))]
    in_vmem = pl.BlockSpec(memory_space=pltpu.VMEM)
    outs = (jax.ShapeDtypeStruct((64, 256), BF16), jax.ShapeDtypeStruct((16, 64), BF16),
            jax.ShapeDtypeStruct((8, 128), F32))
    call = pl.pallas_call(
        functools.partial(kernel, tuple(mesh.axis_names), stop),
        out_shape=outs,
        in_specs=[pl.BlockSpec(memory_space=pl.ANY)] * 4,
        out_specs=(in_vmem, in_vmem, in_vmem),
        scratch_shapes=scratch,
        compiler_params=pltpu.CompilerParams(collective_id=0, has_side_effects=True),
    )
    pass_on = pl.pallas_call(hand_over, out_shape=outs, in_specs=[in_vmem] * 3, out_specs=(in_vmem,) * 3)

    def device_body(mask_blk, user_shard, item_shard, triples):
        out_user, out_item, loss = pass_on(*call(mask_blk, user_shard.T, item_shard, triples.T))
        return out_user.T, out_item, loss.reshape(-1)

    return jax.shard_map(
        device_body,
        mesh=mesh,
        in_specs=(P("row", "col"), P(("row", "col"), None), P(("col", "row"), None), P()),
        out_specs=(P(("row", "col"), None), P(("col", "row"), None), P()),
        check_vma=False,
    )
```

time: 1050 us -> 74 us (0.07)
  blocking collectives: 720 us -> 0 us
  waiting for transfers between devices: 281 us -> 0 us
  Pallas kernels: 0 us -> 73.2 us
  between operations: 14.7 us -> 0.64 us
  other arithmetic: 13.5 us -> 0 us
    unnamed x2 -> x0, blocking collectives: 509 us -> none
    psum x1 -> x0, waiting for transfers between devices: 265 us -> none  [device_body(): picked = lax.psum(picked, ('row', 'col'))]
    all_gather x6 -> x0, blocking collectives: 183 us -> none  [the longest x3 155 us: device_body(): item_panel = lax.all_gather(cur_item, 'row', axis=0, tiled=True)]
    pallas_call x0 -> x2, Pallas kernels: none -> 73.2 us  [the longest x1 71.8 us: device_body(): call(mask_blk, user_shard.T, item_shard, triples.T)]
    psum x2 -> x0, blocking collectives: 27.9 us -> none  [the longest x1 20.8 us: device_body(): deg_item = lax.psum(jnp.sum(mask_blk, axis=0), 'row')]
    reduce_scatter x3 -> x0, waiting for transfers between devices: 15.9 us -> none  [device_body(): lax.psum_scatter(user_part, 'col', scatter_dimension=0, tiled=True)]
  transfers between devices with their start and end apart: 4 -> 0, of which waited for: 3 -> 0; matrix products, arithmetic and copies ran while one was open for 1% -> 0% of each run, Pallas kernels for 0% -> 0%
where the time goes in v2:
time: 74 us; the launch traced here: 73.8 us
  Pallas kernels  73.2 us (99%)
    pallas_call x1, Pallas kernels, device_body(): call(mask_blk, user_shard.T, item_shard, triples.T)  71.8 us

profile of v2, /device:TPU:1, one launch (start us, length us, event | category | flops | bytes accessed | tf_op | source)
XLA Modules:
  0.0 73.8 jit_solution(14037724270961762044)
XLA Ops:
  0.6 71.8 %shard_map.67 = (bf16[64,256]{1,0:T(8,128)(2,1)}, bf16[16,64]{1,0:T(8,128)(2,1)}, f32[8,128]{1,0:T(8,128)}) custom-call(s32[1024,1024]{1,0:T(8,128)} %mask_hbm.1, bf16[64,256]{1,0:T(8,128)(2,1)} %bitcast.4, bf16[16,64]{1,0:T(8,128)(2,1)} %item_hbm.1, s32[3,1024]{1,0:T(4,128)} %bitcast.5), custom_call_target="tpu_custom_call" | custom-call | tf_op jit(solution)/shard_map/pallas_call | solution.py:405
  72.4 1.4 %shard_map.68 = (bf16[64,256]{1,0:T(8,128)(2,1)}, bf16[16,64]{1,0:T(8,128)(2,1)}, f32[8,128]{1,0:T(8,128)}) custom-call(bf16[64,256]{1,0:T(8,128)(2,1)} %get-tuple-element.9.user_in, bf16[16,64]{1,0:T(8,128)(2,1)} %get-tuple-element.10.item_in, f32[8,128]{1,0:T(8,128)} %get-tuple-element.11.loss_in), custom_call_target="tpu_custom_call" | custom-call | tf_op jit(solution)/shard_map/pallas_call | solution.py:405

commit v3 on v2

--- a/solution.py
+++ b/solution.py
@@ -9,6 +9,7 @@
 
 LAYERS = 3
 LANES = 128
+LOADS = 8
 F32 = jnp.float32
 BF16 = jnp.bfloat16
 I32 = jnp.int32
@@ -35,13 +36,13 @@
     *[(Y, (64, 128), F32)] * 3, *[(Z, (32, 128), F32)] * 3, *[(YP, (32, 128), BF16)] * 3,
 )
 SCRATCH = (
-    ((1024, 1024), I32), ((1024, 1024), BF16), ((1024, 1024), BF16),
+    ((1024, 1024), I32), ((1024, 1024), F32), ((1024, 1024), BF16),
     ((1024, 1024), BF16), ((1024, 1024), BF16), ((1024, 128), BF16),
     ((1024, 128), F32), ((8, 1024), F32), ((3, 8, 1024), I32),
     ((5, 8, 128), F32), ((64, 128), BF16), ((3, 64, 256), BF16),
     ((3, 4, 64, 256), F32), ((3, 8, 64, 128), F32),
     ((3, 64, 128), F32), ((3, 32, 128), BF16),
-    ((64, 256), BF16), ((16, 64), BF16), ((3, 1024), I32),
+    ((64, 256), BF16), ((16, 64), BF16), ((3, 1024), I32), ((4, 64, 256), F32),
 )
 
 
@@ -60,8 +61,8 @@
 
 
 def kernel(axis_names, stop, mask_hbm, user_hbm, item_hbm, trip_hbm, out_user_ref, out_item_ref, loss_ref, *refs):
-    (mask_v, mask_b, adj, hot_user, hot_item, row_part, su_col, si_row, ids, small, item_tr, user_src,
-     part_user, part_item, own_item, out_half, user_ref, item_ref, trip_ref) = refs[:len(SCRATCH)]
+    (mask_v, mask_su, adj, hot_user, hot_item, row_part, su_col, si_row, ids, small, item_tr, user_src,
+     part_user, part_item, own_item, out_half, user_ref, item_ref, trip_ref, picked) = refs[:len(SCRATCH)]
     slots = refs[len(SCRATCH):-3]
     load_sem, send_sem, recv_sem = refs[-3:]
     row = lax.axis_index("row")
@@ -147,6 +148,12 @@
         return cp
 
     def body():
+        for q in range(LOADS):
+            rows = pl.ds(q * (1024 // LOADS), 1024 // LOADS)
+            load(mask_hbm.at[rows], mask_v.at[rows])
+        user_cp = load(user_hbm, user_ref)
+        item_cp = load(item_hbm, item_ref)
+        trip_cp = load(trip_hbm, trip_ref)
         barrier = pltpu.get_barrier_semaphore()
         n_peers = 0
         for group in (Z, XYC, YP):
@@ -155,12 +162,6 @@
                     pl.semaphore_signal(barrier, inc=1, device_id=device(group, idx),
                                         device_id_type=pl.DeviceIdType.MESH)
                     n_peers += 1
-        for q in range(4):
-            rows = pl.ds(q * 256, 256)
-            load(mask_hbm.at[rows], mask_v.at[rows])
-        user_cp = load(user_hbm, user_ref)
-        item_cp = load(item_hbm, item_ref)
-        trip_cp = load(trip_hbm, trip_ref)
 
         if stop == 0:
             pl.semaphore_wait(barrier, n_peers)
@@ -171,7 +172,6 @@
         def degree_rows(blk, acc):
             base = pl.multiple_of(blk * 32, 32)
             m = mask_v[pl.ds(base, 32), :].astype(F32)
-            mask_b[pl.ds(base, 32), :] = m.astype(BF16)
             part = m[:, lanes(0)]
             for k in range(1, 8):
                 part = part + m[:, lanes(k)]
@@ -179,9 +179,10 @@
             return acc + ((m[0:8] + m[8:16]) + (m[16:24] + m[24:32]))
 
         acc = jnp.zeros((8, 1024), F32)
-        for q in range(4):
+        trips = 32 // LOADS
+        for q in range(LOADS):
             loads[q].wait()
-            acc = lax.fori_loop(q * 8, (q + 1) * 8, degree_rows, acc)
+            acc = lax.fori_loop(q * trips, (q + 1) * trips, degree_rows, acc)
         col_sum = jnp.sum(acc, axis=0, keepdims=True)
         for k in range(8):
             small[0, k:k + 1, :] = col_sum[:, lanes(k)]
@@ -251,6 +252,15 @@
         scale_user = lax.rsqrt(jnp.maximum(total(DEG_USER), 1.0))
         for k in range(8):
             su_col[pl.ds(k * LANES, LANES), :] = jnp.transpose(jnp.broadcast_to(scale_user[k:k + 1, :], (LANES, LANES)))
+
+        def scale_rows(blk, carry):
+            base = pl.multiple_of(blk * 32, 32)
+            su = su_col[pl.ds(base, 32), :]
+            for k in range(8):
+                mask_su[pl.ds(base, 32), lanes(k)] = mask_v[pl.ds(base, 32), lanes(k)].astype(F32) * su
+            return carry
+
+        lax.fori_loop(0, 32, scale_rows, 0)
         lax.fori_loop(0, 64, one_hot, 0)
         arrive(EMB_USER)
         mark(4)
@@ -263,16 +273,13 @@
             si = si_row[:, cols]
 
             def build(blk, carry):
-                base = pl.multiple_of(blk * 16, 16)
-                su = su_col[pl.ds(base, 16), :]
-                m = mask_b[pl.ds(base, 16), cols].astype(F32)
-                for k in range(2):
-                    si2 = jnp.concatenate([si[:, lanes(k)]] * 2, axis=0)
-                    val = ((m[:, lanes(k)] * su) * si2).astype(BF16)
-                    adj[pl.ds(base, 16), pl.ds(pl.multiple_of(cols.start + k * LANES, LANES), LANES)] = val
+                base = pl.multiple_of(blk * 128, 128)
+                for k in range(8):
+                    rows = pl.ds(pl.multiple_of(base + k * 16, 16), 16)
+                    adj[rows, cols] = (mask_su[rows, cols] * jnp.concatenate([si, si], axis=0)).astype(BF16)
                 return carry
 
-            lax.fori_loop(0, 64, build, 0)
+            lax.fori_loop(0, 8, build, 0)
 
         def user_products(layer, item_panel):
             buf = part_user.at[layer - 1]
@@ -320,36 +327,40 @@
         item_mid(1)
         mark(7)
         tot_user = user_end(1, tot_user)
+        tot_item = item_end(1, tot_item)
+        mark(8)
         arrive(UAG + 1)
         item_columns(IRS + 2, 2, panel(UAG + 1))
-        mark(8)
-        tot_item = item_end(1, tot_item)
         mark(9)
-        item_mid(2)
         arrive(IAG + 1)
         user_products(2, panel(IAG + 1))
         mark(10)
-        tot_item = item_end(2, tot_item)
+        item_mid(2)
         tot_user = user_end(2, tot_user)
         mark(11)
+        tot_item = item_end(2, tot_item)
         arrive(UAG + 2)
         item_columns(IRS + 3, 3, panel(UAG + 2))
         mark(12)
+        item_mid(3)
         arrive(IAG + 2)
         user_products(3, panel(IAG + 2))
-        item_mid(3)
         mark(13)
+        item_end(3, tot_item)
         user_end(3, tot_user)
         out_user_ref[...] = user_src[2]
         arrive(UAG + 3)
-        picked_user = mm(panel(UAG + 3), hot_user[...], NN)
-        item_end(3, tot_item)
+        out_panel = panel(UAG + 3)
+        for k in range(4):
+            picked[k] = mm(out_panel, hot_user[:, k * 256:(k + 1) * 256], NN)
         mark(14)
         arrive(IAG + 3)
-        picked_item = mm(panel(IAG + 3), hot_item[...], NN)
-        red = jnp.sum(picked_user * picked_item, axis=0, keepdims=True)
-        for k in range(8):
-            small[3, k:k + 1, :] = red[:, lanes(k)]
+        out_panel = panel(IAG + 3)
+        for k in range(4):
+            prod = mm(out_panel, hot_item[:, k * 256:(k + 1) * 256], NN) * picked[k]
+            red = jnp.sum(prod, axis=0, keepdims=True)
+            small[3, 2 * k:2 * k + 1, :] = red[:, lanes(0)]
+            small[3, 2 * k + 1:2 * k + 2, :] = red[:, lanes(1)]
         slots[LOSS_A][col * 8 + pos] = small[3]
         send_all(LOSS_A, small.at[3])
         mark(15)
@@ -377,32 +388,40 @@
         whole(stage).wait_send()
 
 
-def hand_over(user_in, item_in, loss_in, user_out, item_out, loss_out):
-    user_out[...] = user_in[...]
-    item_out[...] = item_in[...]
-    loss_out[...] = loss_in[...]
+def hand_over(user_in, item_in, loss_in, user_out, item_out, loss_out, sems):
+    pairs = ((user_in, user_out), (item_in, item_out), (loss_in, loss_out))
+    copies = [pltpu.make_async_copy(src, dst, sems.at[k]) for k, (src, dst) in enumerate(pairs)]
+    for cp in copies:
+        cp.start()
+    for cp in copies:
+        cp.wait()
 
 
 def solution(mesh, stop=None):
     scratch = [pltpu.VMEM(*spec) for spec in SCRATCH]
     scratch += [pltpu.VMEM((SIZE[group],) + shape, dtype) for group, shape, dtype in STAGES]
-    scratch += [pltpu.SemaphoreType.DMA((7,)), pltpu.SemaphoreType.DMA((len(STAGES),)),
+    scratch += [pltpu.SemaphoreType.DMA((LOADS + 3,)), pltpu.SemaphoreType.DMA((len(STAGES),)),
                 pltpu.SemaphoreType.DMA((len(STAGES),))]
     in_vmem = pl.BlockSpec(memory_space=pltpu.VMEM)
     outs = (jax.ShapeDtypeStruct((64, 256), BF16), jax.ShapeDtypeStruct((16, 64), BF16),
             jax.ShapeDtypeStruct((8, 128), F32))
     call = pl.pallas_call(
         functools.partial(kernel, tuple(mesh.axis_names), stop),
-        out_shape=outs,
+        out_shape=tuple(pltpu.VMEM(out.shape, out.dtype) for out in outs),
         in_specs=[pl.BlockSpec(memory_space=pl.ANY)] * 4,
         out_specs=(in_vmem, in_vmem, in_vmem),
         scratch_shapes=scratch,
         compiler_params=pltpu.CompilerParams(collective_id=0, has_side_effects=True),
     )
-    pass_on = pl.pallas_call(hand_over, out_shape=outs, in_specs=[in_vmem] * 3, out_specs=(in_vmem,) * 3)
+    pass_on = pl.pallas_call(
+        hand_over, out_shape=outs, in_specs=[in_vmem] * 3,
+        out_specs=(pl.BlockSpec(memory_space=pl.ANY),) * 3,
+        scratch_shapes=[pltpu.SemaphoreType.DMA((3,))],
+    )
 
     def device_body(mask_blk, user_shard, item_shard, triples):
-        out_user, out_item, loss = pass_on(*call(mask_blk, user_shard.T, item_shard, triples.T))
+        held = call(mask_blk, user_shard.T, item_shard, triples.T)
+        out_user, out_item, loss = pass_on(*[pltpu.with_memory_space_constraint(x, pltpu.VMEM) for x in held])
         return out_user.T, out_item, loss.reshape(-1)
 
     return jax.shard_map(

time: 74 us -> 69.6 us (0.941)
  Pallas kernels: 73.2 us -> 68.8 us
    pallas_call x2, Pallas kernels: 73.2 us -> 68.8 us  [the longest x1 68.2 us: device_body(): held = call(mask_blk, user_shard.T, item_shard, triples.T)]
where the time goes in v3:
time: 69.6 us; the launch traced here: 69.5 us
  Pallas kernels  68.8 us (99%)
    pallas_call x1, Pallas kernels, device_body(): held = call(mask_blk, user_shard.T, item_shard, triples.T)  68.2 us

profile of v3, /device:TPU:1, one launch (start us, length us, event | category | flops | bytes accessed | tf_op | source)
XLA Modules:
  0.0 69.5 jit_solution(6170621541837295348)
XLA Ops:
  0.6 68.2 %shard_map.67 = (bf16[64,256]{1,0:T(8,128)(2,1)S(1)}, bf16[16,64]{1,0:T(8,128)(2,1)S(1)}, f32[8,128]{1,0:T(8,128)S(1)}) custom-call(s32[1024,1024]{1,0:T(8,128)} %mask_hbm.1, bf16[64,256]{1,0:T(8,128)(2,1)} %bitcast.4, bf16[16,64]{1,0:T(8,128)(2,1)} %item_hbm.1, s32[3,1024]{1,0:T(4,128)} %bitcast.5), custom_call_target="tpu_custom_call" | custom-call | tf_op jit(solution)/shard_map/pallas_call | solution.py:423
  68.8 0.6 shard_map.68

commit v4 on v3

v4 whole, which is shorter than its diff:
```python
import functools

import jax
import jax.numpy as jnp
from jax import lax
from jax.experimental import pallas as pl
from jax.experimental.pallas import tpu as pltpu
from jax.sharding import PartitionSpec as P

LAYERS = 3
LANES = 128
LOADS = 8
F32 = jnp.float32
BF16 = jnp.bfloat16
I32 = jnp.int32
NT = (((1,), (1,)), ((), ()))
NN = (((1,), (0,)), ((), ()))

DX = (2, 1, 3, 0)
DY = (2, 1, 3, 0)
DZ = (4, 3, 5, 2, 6, 1, 7, 0)
EVERY = ((3, 3), (3, 3))
PLANE = ((7, 7), (7, 7))
GATHER = ((0, 7), (4, 3))
SPREAD = ((8, 7), (0, 15))
ROW = (8, LANES)
HALF = (64, LANES)
QUARTER = (32, LANES)
BLOCK = (64, 256)
STAGES = (
    (4, ROW, F32, *EVERY), (8, ROW, F32, *GATHER), (8, ROW, F32, *SPREAD),
    (4, BLOCK, BF16, *EVERY), (8, (16, 64), BF16, *PLANE), (8, HALF, BF16, *PLANE),
    (1, BLOCK, BF16, (0, 1), (1, 0)), (32, ROW, F32, (0, 31), (16, 15)), (8, ROW, F32, *SPREAD),
    *[(8, HALF, F32, *GATHER)] * 6,
    *[(4, HALF, BF16, (4, 3), (0, 7))] * 6,
    *[(8, HALF, F32, *GATHER)] * 6,
    *[(8, QUARTER, F32, (0, 7), (0, 7))] * 6,
    *[(8, QUARTER, BF16, *SPREAD)] * 6,
)
(DEG_USER, DEG_ITEM_A, DEG_ITEM_B, EMB_USER, EMB_ITEM_A, EMB_ITEM_B, EMB_MATE, LOSS_A, LOSS_Z) = range(9)
URS, UAG, IRS, IZZ, IAG = range(7, 37, 6)


def layer_stage(kind, layer, half):
    return kind + 2 * layer + half


SQUARE = (1024, 1024)
SCRATCH = (
    (SQUARE, I32), (SQUARE, F32), (SQUARE, BF16), (SQUARE, BF16), (SQUARE, BF16), ((1024, LANES), BF16),
    ((1024, LANES), F32), ((8, 1024), F32), ((3, 8, 1024), I32), ((5, *ROW), F32), (HALF, BF16),
    ((6, 2, *HALF), BF16), ((6, 4, *HALF), F32), ((6, 4, *HALF), F32), ((6, *HALF), F32), ((6, *QUARTER), BF16),
    (BLOCK, BF16), ((16, 64), BF16), ((3, 1024), I32), ((4, *BLOCK), F32),
    ((2, 2, *HALF), F32), ((2, *QUARTER), F32),
)


def mm(lhs, rhs, dims):
    return lax.dot_general(lhs, rhs, dims, preferred_element_type=F32)


def eye(rows, cols):
    row_id = lax.broadcasted_iota(I32, (rows, cols), 0)
    col_id = lax.broadcasted_iota(I32, (rows, cols), 1)
    return jnp.where(row_id == col_id, 1.0, 0.0).astype(BF16)


def kernel(axis_names, mask_hbm, user_hbm, item_hbm, trip_hbm, out_user_ref, out_item_ref, loss_ref, *refs):
    (mask_v, mask_su, adj, hot_user, hot_item, row_part, su_col, si_row, ids, small, item_tr, user_src,
     part_user, part_item, own_item, out_half, user_ref, item_ref, trip_ref, picked,
     tot_user, tot_item) = refs[:len(SCRATCH)]
    slots = refs[len(SCRATCH):-3]
    load_sem, send_sem, recv_sem = refs[-3:]
    row = lax.axis_index("row")
    col = lax.axis_index("col")
    zed = row // 8
    pos = row % 8
    yy = pos // 2
    core = pos % 2
    par = zed % 2
    started, arrived, loads = [], [], []

    def only(which):
        return pl.when(core == which)

    def device(to_col, to_row):
        return tuple(to_col if name == "col" else to_row for name in axis_names)

    def at_x(dx, which=None):
        return (col + dx) % 4, row if which is None else row - core + which

    def at_y(dy, which):
        return col, zed * 8 + (yy + dy) % 4 * 2 + which

    def at_z(dz, which=None):
        return col, (zed + dz) % 8 * 8 + (pos if which is None else yy * 2 + which)

    def send(stage, slot, src, target):
        if stage not in started:
            started.append(stage)
        pltpu.make_async_remote_copy(
            src_ref=src, dst_ref=slots[stage].at[slot],
            send_sem=send_sem.at[stage], recv_sem=recv_sem.at[stage],
            device_id=device(*target), device_id_type=pl.DeviceIdType.MESH).start()

    def batch(stage, count):
        part = slots[stage].at[pl.ds(0, count)]
        return pltpu.make_async_remote_copy(
            src_ref=part, dst_ref=part, send_sem=send_sem.at[stage], recv_sem=recv_sem.at[stage],
            device_id=device(*at_x(1)), device_id_type=pl.DeviceIdType.MESH)

    def arrive(stage):
        arrived.append(stage)
        count = STAGES[stage][3]
        if count[0] == count[1]:
            batch(stage, count[0]).wait_recv()
        else:
            for which in (0, 1):
                if count[which]:
                    only(which)(batch(stage, count[which]).wait_recv)

    def arrive_one(stage):
        arrived.append(stage)
        batch(stage, STAGES[stage][3][1]).wait_recv()

    def sent(stage, which):
        left = STAGES[stage][4][which]
        while left:
            count = min(left, STAGES[stage][0])
            batch(stage, count).wait_send()
            left -= count

    def total(stage, first=0, last=None):
        buf = slots[stage]
        acc = buf[first]
        for idx in range(first + 1, last or STAGES[stage][0]):
            acc = acc + buf[idx]
        return acc

    def panel(stage):
        buf = slots[stage]
        return jnp.concatenate([buf[idx] for idx in range(STAGES[stage][0])], axis=1)

    def columns(kind, layer, picks):
        bufs = [slots[layer_stage(kind, layer, half)] for half in (0, 1)]
        return jnp.concatenate([buf[idx] for idx in picks for buf in bufs], axis=1)

    def user_panel(layer):
        return columns(UAG, layer, range(4))

    def item_panel(layer):
        return jnp.concatenate([columns(IAG, layer, range(4)), columns(IAG, layer, range(4, 8))], axis=0)

    def arrive_both(kind, layer):
        for half in (0, 1):
            arrive(layer_stage(kind, layer, half))

    def lanes(k):
        return slice(k * LANES, (k + 1) * LANES)

    def load(src, dst):
        cp = pltpu.make_async_copy(src, dst, load_sem.at[len(loads)])
        cp.start()
        loads.append(cp)
        return cp

    def to_owners(stage, slot, src, local):
        for dy in DY[:3]:
            send(stage, slot, src, at_y(dy, 1))
        only(0)(lambda: send(stage, slot, src, at_y(0, 1)))

        @only(1)
        def _():
            slots[stage][slot] = local

    def along_z(stage, src):
        for dz in DZ:
            for which in (0, 1):
                if dz or not which:
                    send(stage, zed, src, at_z(dz, which))

    def body():
        for q in range(LOADS):
            rows = pl.ds(q * (1024 // LOADS), 1024 // LOADS)
            load(mask_hbm.at[rows], mask_v.at[rows])
        user_cp = load(user_hbm, user_ref)
        item_cp = load(item_hbm, item_ref)
        trip_cp = load(trip_hbm, trip_ref)
        barrier = pltpu.get_barrier_semaphore()
        targets = [at_z(dz, which) for dz in DZ[:7] for which in (0, 1)]
        targets += [((col + dx) % 4, zed * 8 + (pos + off) % 8) for dx in DX for off in range(8) if dx or off]
        targets += [(col, (zed - par + 1 - par) * 8 + (yy + dy) % 4 * 2 + which) for dy in DY[:3] for which in (0, 1)]
        for target in targets:
            pl.semaphore_signal(barrier, inc=1, device_id=device(*target), device_id_type=pl.DeviceIdType.MESH)
        n_peers = len(targets)


        def degree_rows(blk, acc):
            base = pl.multiple_of(blk * 32, 32)
            m = mask_v[pl.ds(base, 32), :].astype(F32)
            part = m[:, lanes(0)]
            for k in range(1, 8):
                part = part + m[:, lanes(k)]
            row_part[pl.ds(base, 32), :] = part.astype(BF16)
            return acc + ((m[0:8] + m[8:16]) + (m[16:24] + m[24:32]))

        acc = jnp.zeros((8, 1024), F32)
        trips = 32 // LOADS
        for q in range(LOADS):
            loads[q].wait()
            acc = lax.fori_loop(q * trips, (q + 1) * trips, degree_rows, acc)
        col_sum = jnp.sum(acc, axis=0, keepdims=True)
        for k in range(8):
            small[0, k:k + 1, :] = col_sum[:, lanes(k)]
        row_sum = mm(jnp.ones((8, LANES), BF16), row_part[...], NT)
        for k in range(8):
            small[1, k:k + 1, :] = row_sum[0:1, lanes(k)]
        slots[DEG_USER][col] = small[1]
        for cp in (user_cp, item_cp, trip_cp):
            cp.wait()
        pl.semaphore_wait(barrier, n_peers)
        to_owners(DEG_ITEM_A, pos, small.at[0], small[0])
        for dx in DX[:3]:
            send(DEG_USER, col, small.at[1], at_x(dx))
        for dx in DX[:3]:
            send(EMB_USER, col, user_ref, at_x(dx))
        for off in (4, 5, 3, 2, 6, 7, 1):
            send(EMB_ITEM_A, pos, item_ref, (col, zed * 8 + (pos + off) % 8))
        only(0)(lambda: send(EMB_MATE, 0, user_ref, at_y(0, 1)))
        user_t = user_ref[...]
        slots[EMB_USER][col] = user_t
        slots[EMB_ITEM_A][pos] = item_ref[...]
        for k, block in enumerate((row, col, col)):
            ids[k] = jnp.broadcast_to(trip_ref[k:k + 1, :] - block * 1024, (8, 1024))

        def one_hot(blk, carry):
            base = pl.multiple_of(blk * 16, 16)
            for k in range(8):
                hits = []
                for half in range(2):
                    sub = lax.broadcasted_iota(I32, (8, LANES), 0) + (base + half * 8)
                    hits.append([jnp.where(ids[w, :, lanes(k)] == sub, 1.0, 0.0) for w in range(3)])
                hot_user[pl.ds(base, 16), lanes(k)] = jnp.concatenate([hit[0] for hit in hits], axis=0).astype(BF16)
                hot_item[pl.ds(base, 16), lanes(k)] = jnp.concatenate([hit[1] - hit[2] for hit in hits], axis=0).astype(BF16)
            return carry

        def spread_halves(kind, layer, slot, store, offsets, product, target):
            for off in offsets:
                res = product(off)
                for half in (0, 1):
                    buf = store.at[2 * (layer - 1) + half]
                    if off:
                        buf[off] = res[:, lanes(half)]
                        if not half:
                            send(layer_stage(kind, layer, half), slot, buf.at[off], target(off))
                    else:
                        @only(0)
                        def _():
                            buf[off] = res[:, lanes(half)]
                            if not half:
                                send(layer_stage(kind, layer, half), slot, buf.at[off], target(off))

                        @only(1)
                        def _():
                            slots[layer_stage(kind, layer, half)][slot] = res[:, lanes(half)]
            stage = layer_stage(kind, layer, 1)
            buf = store.at[2 * layer - 1]
            for off in offsets[:3]:
                send(stage, slot, buf.at[off], target(off))
            only(0)(lambda: send(stage, slot, buf.at[0], target(0)))

        def item_columns(layer, user_rows, prepare=None):
            def product(off):
                cols = pl.ds(pl.multiple_of((yy + off) % 4 * 256, 256), 256)
                if prepare is not None:
                    prepare(cols)
                return mm(user_rows, adj[:, cols], NN)

            spread_halves(IRS, layer, pos, part_item, DY, product, lambda off: at_y(off, 1))

        def user_products(layer, item_rows):
            def product(off):
                rows = pl.ds(pl.multiple_of((col + off) % 4 * 256, 256), 256)
                return mm(item_rows, adj[rows, :], NT)

            spread_halves(URS, layer, core * 4 + col, part_user, DX, product, lambda off: at_x(off, 1))

        @only(1)
        def _():
            arrive_one(DEG_ITEM_A)
            deg_sum = total(DEG_ITEM_A)
            small[2] = deg_sum
            slots[DEG_ITEM_B][zed] = deg_sum
            along_z(DEG_ITEM_B, small.at[2])

        arrive(EMB_ITEM_A)
        gathered = jnp.concatenate([slots[EMB_ITEM_A][k] for k in range(8)], axis=0)
        item_t = mm(eye(64, 64), gathered, NT).astype(BF16)
        item_tr[...] = item_t
        slots[EMB_ITEM_B][zed] = item_t
        for dz in DZ[:7]:
            send(EMB_ITEM_B, zed, item_tr, at_z(dz))
        arrive(DEG_USER)
        scale_user = lax.rsqrt(jnp.maximum(total(DEG_USER), 1.0))
        for k in range(8):
            su_col[pl.ds(k * LANES, LANES), :] = jnp.transpose(jnp.broadcast_to(scale_user[k:k + 1, :], (LANES, LANES)))

        def scale_rows(blk, carry):
            base = pl.multiple_of(blk * 32, 32)
            su = su_col[pl.ds(base, 32), :]
            for k in range(8):
                mask_su[pl.ds(base, 32), lanes(k)] = mask_v[pl.ds(base, 32), lanes(k)].astype(F32) * su
            return carry

        lax.fori_loop(0, 32, scale_rows, 0)
        lax.fori_loop(0, 64, one_hot, 0)
        arrive(EMB_USER)
        arrive(DEG_ITEM_B)
        scale_item = lax.rsqrt(jnp.maximum(total(DEG_ITEM_B), 1.0))
        for k in range(8):
            si_row[:, lanes(k)] = jnp.broadcast_to(scale_item[k:k + 1, :], (8, LANES))

        def prepare(cols):
            si = si_row[:, cols]

            def build(blk, carry):
                base = pl.multiple_of(blk * 128, 128)
                for k in range(8):
                    rows = pl.ds(pl.multiple_of(base + k * 16, 16), 16)
                    adj[rows, cols] = (mask_su[rows, cols] * jnp.concatenate([si, si], axis=0)).astype(BF16)
                return carry

            lax.fori_loop(0, 8, build, 0)

        def item_mid(layer, half):
            @only(1)
            def _():
                own = own_item.at[2 * (layer - 1) + half]
                stage = layer_stage(IRS, layer, half)
                arrive_one(stage)
                own[...] = total(stage)
                stage = layer_stage(IZZ, layer, half)
                for dz in DZ[:7]:
                    dims = pl.ds(pl.multiple_of((par + dz) % 2 * 32, 32), 32)
                    send(stage, zed, own.at[dims], at_z(dz))
                slots[stage][zed] = own[pl.ds(pl.multiple_of(par * 32, 32), 32)]

        def finish(val, tot, layer):
            tot[...] = tot[...] + val.astype(F32)
            return val if layer < LAYERS else (tot[...] * 0.25).astype(BF16)

        def user_end(layer, half):
            @only(1)
            def _():
                keep = user_src.at[2 * (layer - 1) + half]
                come = layer_stage(URS, layer, half)
                stage = layer_stage(UAG, layer, half)
                arrive_one(come)
                for which in (0, 1):
                    val = total(come, 4 * which, 4 * which + 4).astype(BF16)
                    res = finish(val, tot_user.at[which, half], layer)
                    keep[which] = res
                    for dx in DX:
                        if dx or not which:
                            send(stage, col, keep.at[which], at_x(dx, which))
                slots[stage][col] = res

        def item_end(layer, half):
            @only(1)
            def _():
                keep = out_half.at[2 * (layer - 1) + half]
                mine = par * 4 + yy
                come = layer_stage(IZZ, layer, half)
                stage = layer_stage(IAG, layer, half)
                arrive_one(come)
                res = finish(total(come).astype(BF16), tot_item.at[half], layer)
                keep[...] = res
                for plane in (zed - par + 1 - par, zed):
                    for dy in DY:
                        for which in (0, 1):
                            if plane is not zed or dy or not which:
                                send(stage, mine, keep, (col, plane * 8 + (yy + dy) % 4 * 2 + which))
                slots[stage][mine] = res

        item_columns(1, panel(EMB_USER), prepare)
        arrive(EMB_ITEM_B)
        user_products(1, panel(EMB_ITEM_B))

        @only(1)
        def _():
            arrive_one(EMB_MATE)
            dims = pl.ds(pl.multiple_of(par * 32, 32), 32)
            for half in (0, 1):
                tot_user[0, half] = slots[EMB_MATE][0, :, lanes(half)].astype(F32)
                tot_user[1, half] = user_t[:, lanes(half)].astype(F32)
                tot_item[half] = slots[EMB_ITEM_B][2 * yy + half, dims].astype(F32)

        for half in (0, 1):
            item_mid(1, half)
            user_end(1, half)
        for half in (0, 1):
            item_end(1, half)
        arrive_both(UAG, 1)
        item_columns(2, user_panel(1))
        arrive_both(IAG, 1)
        user_products(2, item_panel(1))
        for step in (item_mid, user_end, item_end):
            for half in (0, 1):
                step(2, half)
        arrive_both(UAG, 2)
        item_columns(3, user_panel(2))
        for half in (0, 1):
            item_mid(3, half)
        arrive_both(IAG, 2)
        user_products(3, item_panel(2))
        for step in (item_end, user_end):
            for half in (0, 1):
                step(3, half)
        arrive_both(UAG, 3)
        for half in (0, 1):
            out_user_ref[:, lanes(half)] = slots[layer_stage(UAG, 3, half)][col]
        out_panel = user_panel(3)
        for k in range(4):
            picked[k] = mm(out_panel, hot_user[:, k * 256:(k + 1) * 256], NN)
        arrive_both(IAG, 3)
        out_panel = item_panel(3)
        for k in range(4):
            prod = mm(out_panel, hot_item[:, k * 256:(k + 1) * 256], NN) * picked[k]
            red = jnp.sum(prod, axis=0, keepdims=True)
            small[3, 2 * k:2 * k + 1, :] = red[:, lanes(0)]
            small[3, 2 * k + 1:2 * k + 2, :] = red[:, lanes(1)]
        place = col * 8 + pos
        for dx in DX:
            for dy in DY:
                target = ((col + dx) % 4, zed * 8 + (yy + dy) % 4 * 2 + 1)
                if dx or dy:
                    send(LOSS_A, place, small.at[3], target)
                else:
                    only(0)(lambda: send(LOSS_A, place, small.at[3], target))

        @only(1)
        def _():
            slots[LOSS_A][place] = small[3]

        @only(1)
        def _():
            arrive_one(LOSS_A)
            val = total(LOSS_A)
            small[4] = val
            slots[LOSS_Z][zed] = val
            along_z(LOSS_Z, small.at[4])

        row_id = lax.broadcasted_iota(I32, (16, LANES), 0) + pos * 16
        col_id = lax.broadcasted_iota(I32, (16, LANES), 1)
        pick = jnp.where(row_id == col_id, 1.0, 0.0).astype(BF16)

        for half in (0, 1):
            @pl.when(par == half)
            def _():
                buf = slots[layer_stage(IAG, 3, half)]
                block = jnp.concatenate([buf[zed // 2], buf[4 + zed // 2]], axis=0)
                out_item_ref[...] = mm(pick, block, NT).astype(BF16)

        arrive(LOSS_Z)
        neg = -total(LOSS_Z)
        loss_ref[...] = jnp.maximum(neg, 0.0) + jnp.log1p(jnp.exp(-jnp.abs(neg)))

    body()
    for which in (0, 1):
        @only(which)
        def _():
            for stage in started:
                sent(stage, which)


def hand_over(user_in, item_in, loss_in, user_out, item_out, loss_out, sems):
    pairs = ((user_in, user_out), (item_in, item_out), (loss_in, loss_out))
    copies = [pltpu.make_async_copy(src, dst, sems.at[k]) for k, (src, dst) in enumerate(pairs)]
    for cp in copies:
        cp.start()
    for cp in copies:
        cp.wait()


def solution(mesh):
    scratch = [pltpu.VMEM(*spec) for spec in SCRATCH]
    scratch += [pltpu.VMEM((stage[0],) + stage[1], stage[2]) for stage in STAGES]
    scratch += [pltpu.SemaphoreType.DMA((LOADS + 3,)), pltpu.SemaphoreType.DMA((len(STAGES),)),
                pltpu.SemaphoreType.DMA((len(STAGES),))]
    in_vmem = pl.BlockSpec(memory_space=pltpu.VMEM)
    outs = (jax.ShapeDtypeStruct((64, 256), BF16), jax.ShapeDtypeStruct((16, 64), BF16),
            jax.ShapeDtypeStruct((8, 128), F32))
    call = pl.pallas_call(
        functools.partial(kernel, tuple(mesh.axis_names)),
        out_shape=tuple(pltpu.VMEM(out.shape, out.dtype) for out in outs),
        in_specs=[pl.BlockSpec(memory_space=pl.ANY)] * 4,
        out_specs=(in_vmem, in_vmem, in_vmem),
        scratch_shapes=scratch,
        compiler_params=pltpu.CompilerParams(collective_id=0, has_side_effects=True),
    )
    pass_on = pl.pallas_call(
        hand_over, out_shape=outs, in_specs=[in_vmem] * 3,
        out_specs=(pl.BlockSpec(memory_space=pl.ANY),) * 3,
        scratch_shapes=[pltpu.SemaphoreType.DMA((3,))],
    )

    def device_body(mask_blk, user_shard, item_shard, triples):
        held = call(mask_blk, user_shard.T, item_shard, triples.T)
        out_user, out_item, loss = pass_on(*[pltpu.with_memory_space_constraint(x, pltpu.VMEM) for x in held])
        return out_user.T, out_item, loss.reshape(-1)

    return jax.shard_map(
        device_body,
        mesh=mesh,
        in_specs=(P("row", "col"), P(("row", "col"), None), P(("col", "row"), None), P()),
        out_specs=(P(("row", "col"), None), P(("col", "row"), None), P()),
        check_vma=False,
    )
```

time: 69.6 us -> 67.6 us (0.971)
  Pallas kernels: 68.8 us -> 66.9 us
    pallas_call x1, Pallas kernels: 68.2 us -> 66.3 us  [device_body(): held = call(mask_blk, user_shard.T, item_shard, triples.T)]
where the time goes in v4:
time: 67.6 us
  Pallas kernels  66.9 us (99%)
    pallas_call x1, Pallas kernels, device_body(): held = call(mask_blk, user_shard.T, item_shard, triples.T)  66.3 us

profile of v4, /device:TPU:1, one launch (start us, length us, event | category | flops | bytes accessed | tf_op | source)
XLA Modules:
  0.0 67.6 jit_solution(597057577947930632)
XLA Ops:
  0.6 66.3 %shard_map.67 = (bf16[64,256]{1,0:T(8,128)(2,1)S(1)}, bf16[16,64]{1,0:T(8,128)(2,1)S(1)}, f32[8,128]{1,0:T(8,128)S(1)}) custom-call(s32[1024,1024]{1,0:T(8,128)} %mask_hbm.1, bf16[64,256]{1,0:T(8,128)(2,1)} %bitcast.4, bf16[16,64]{1,0:T(8,128)(2,1)} %item_hbm.1, s32[3,1024]{1,0:T(4,128)} %bitcast.5), custom_call_target="tpu_custom_call" | custom-call | tf_op jit(solution)/shard_map/pallas_call | solution.py:508
  66.9 0.6 shard_map.68

commit v5 on v4

--- a/solution.py
+++ b/solution.py
@@ -50,7 +50,7 @@
     (SQUARE, I32), (SQUARE, F32), (SQUARE, BF16), (SQUARE, BF16), (SQUARE, BF16), ((1024, LANES), BF16),
     ((1024, LANES), F32), ((8, 1024), F32), ((3, 8, 1024), I32), ((5, *ROW), F32), (HALF, BF16),
     ((6, 2, *HALF), BF16), ((6, 4, *HALF), F32), ((6, 4, *HALF), F32), ((6, *HALF), F32), ((6, *QUARTER), BF16),
-    (BLOCK, BF16), ((16, 64), BF16), ((3, 1024), I32), ((4, *BLOCK), F32),
+    (BLOCK, BF16), ((16, 64), BF16), ((3, 1024), I32), ((4, *BLOCK), F32), ((4, *BLOCK), F32),
     ((2, 2, *HALF), F32), ((2, *QUARTER), F32),
 )
 
@@ -67,7 +67,7 @@
 
 def kernel(axis_names, mask_hbm, user_hbm, item_hbm, trip_hbm, out_user_ref, out_item_ref, loss_ref, *refs):
     (mask_v, mask_su, adj, hot_user, hot_item, row_part, su_col, si_row, ids, small, item_tr, user_src,
-     part_user, part_item, own_item, out_half, user_ref, item_ref, trip_ref, picked,
+     part_user, part_item, own_item, out_half, user_ref, item_ref, trip_ref, picked, chosen,
      tot_user, tot_item) = refs[:len(SCRATCH)]
     slots = refs[len(SCRATCH):-3]
     load_sem, send_sem, recv_sem = refs[-3:]
@@ -78,7 +78,7 @@
     yy = pos // 2
     core = pos % 2
     par = zed % 2
-    started, arrived, loads = [], [], []
+    loads = []
 
     def only(which):
         return pl.when(core == which)
@@ -96,8 +96,6 @@
         return col, (zed + dz) % 8 * 8 + (pos if which is None else yy * 2 + which)
 
     def send(stage, slot, src, target):
-        if stage not in started:
-            started.append(stage)
         pltpu.make_async_remote_copy(
             src_ref=src, dst_ref=slots[stage].at[slot],
             send_sem=send_sem.at[stage], recv_sem=recv_sem.at[stage],
@@ -110,7 +108,6 @@
             device_id=device(*at_x(1)), device_id_type=pl.DeviceIdType.MESH)
 
     def arrive(stage):
-        arrived.append(stage)
         count = STAGES[stage][3]
         if count[0] == count[1]:
             batch(stage, count[0]).wait_recv()
@@ -120,7 +117,6 @@
                     only(which)(batch(stage, count[which]).wait_recv)
 
     def arrive_one(stage):
-        arrived.append(stage)
         batch(stage, STAGES[stage][3][1]).wait_recv()
 
     def sent(stage, which):
@@ -235,11 +231,13 @@
 
         def one_hot(blk, carry):
             base = pl.multiple_of(blk * 16, 16)
+            base_item = base // 512 * LANES + base % 512 // LANES * 256 + base % LANES
             for k in range(8):
                 hits = []
                 for half in range(2):
-                    sub = lax.broadcasted_iota(I32, (8, LANES), 0) + (base + half * 8)
-                    hits.append([jnp.where(ids[w, :, lanes(k)] == sub, 1.0, 0.0) for w in range(3)])
+                    sub = lax.broadcasted_iota(I32, ROW, 0) + half * 8
+                    near = (sub + base, sub + base_item, sub + base_item)
+                    hits.append([jnp.where(ids[w, :, lanes(k)] == near[w], 1.0, 0.0) for w in range(3)])
                 hot_user[pl.ds(base, 16), lanes(k)] = jnp.concatenate([hit[0] for hit in hits], axis=0).astype(BF16)
                 hot_item[pl.ds(base, 16), lanes(k)] = jnp.concatenate([hit[1] - hit[2] for hit in hits], axis=0).astype(BF16)
             return carry
@@ -375,9 +373,9 @@
                 arrive_one(come)
                 res = finish(total(come).astype(BF16), tot_item.at[half], layer)
                 keep[...] = res
-                for plane in (zed - par + 1 - par, zed):
-                    for dy in DY:
-                        for which in (0, 1):
+                for which in (0, 1):
+                    for plane in (zed - par + 1 - par, zed):
+                        for dy in DY:
                             if plane is not zed or dy or not which:
                                 send(stage, mine, keep, (col, plane * 8 + (yy + dy) % 4 * 2 + which))
                 slots[stage][mine] = res
@@ -395,9 +393,9 @@
                 tot_user[1, half] = user_t[:, lanes(half)].astype(F32)
                 tot_item[half] = slots[EMB_ITEM_B][2 * yy + half, dims].astype(F32)
 
-        for half in (0, 1):
-            item_mid(1, half)
-            user_end(1, half)
+        for step in (item_mid, user_end):
+            for half in (0, 1):
+                step(1, half)
         for half in (0, 1):
             item_end(1, half)
         arrive_both(UAG, 1)
@@ -409,11 +407,11 @@
                 step(2, half)
         arrive_both(UAG, 2)
         item_columns(3, user_panel(2))
+        arrive_both(IAG, 2)
+        user_products(3, item_panel(2))
         for half in (0, 1):
             item_mid(3, half)
-        arrive_both(IAG, 2)
-        user_products(3, item_panel(2))
-        for step in (item_end, user_end):
+        for step in (user_end, item_end):
             for half in (0, 1):
                 step(3, half)
         arrive_both(UAG, 3)
@@ -422,13 +420,21 @@
         out_panel = user_panel(3)
         for k in range(4):
             picked[k] = mm(out_panel, hot_user[:, k * 256:(k + 1) * 256], NN)
-        arrive_both(IAG, 3)
-        out_panel = item_panel(3)
+        def item_half(half):
+            stage = layer_stage(IAG, LAYERS, half)
+            arrive(stage)
+            rows = [jnp.concatenate([slots[stage][k + idx] for idx in range(4)], axis=1) for k in (0, 4)]
+            return jnp.concatenate(rows, axis=0)
+
+        first = item_half(0)
         for k in range(4):
-            prod = mm(out_panel, hot_item[:, k * 256:(k + 1) * 256], NN) * picked[k]
+            chosen[k] = mm(first, hot_item[:512, k * 256:(k + 1) * 256], NN)
+        second = item_half(1)
+        for k in range(4):
+            prod = (chosen[k] + mm(second, hot_item[512:, k * 256:(k + 1) * 256], NN)) * picked[k]
             red = jnp.sum(prod, axis=0, keepdims=True)
-            small[3, 2 * k:2 * k + 1, :] = red[:, lanes(0)]
-            small[3, 2 * k + 1:2 * k + 2, :] = red[:, lanes(1)]
+            for half in (0, 1):
+                small[3, 2 * k + half:2 * k + half + 1, :] = red[:, lanes(half)]
         place = col * 8 + pos
         for dx in DX:
             for dy in DY:
@@ -461,16 +467,17 @@
                 block = jnp.concatenate([buf[zed // 2], buf[4 + zed // 2]], axis=0)
                 out_item_ref[...] = mm(pick, block, NT).astype(BF16)
 
+        for which in (0, 1):
+            @only(which)
+            def _():
+                for stage in range(len(STAGES)):
+                    sent(stage, which)
+
         arrive(LOSS_Z)
         neg = -total(LOSS_Z)
         loss_ref[...] = jnp.maximum(neg, 0.0) + jnp.log1p(jnp.exp(-jnp.abs(neg)))
 
     body()
-    for which in (0, 1):
-        @only(which)
-        def _():
-            for stage in started:
-                sent(stage, which)
 
 
 def hand_over(user_in, item_in, loss_in, user_out, item_out, loss_out, sems):

time: 67.6 us -> 65.6 us (0.970)
  Pallas kernels: 66.9 us -> 64.9 us
    pallas_call x1, Pallas kernels: 66.3 us -> 64.3 us  [device_body(): held = call(mask_blk, user_shard.T, item_shard, triples.T)]
where the time goes in v5:
time: 65.6 us
  Pallas kernels  64.9 us (99%)
    pallas_call x1, Pallas kernels, device_body(): held = call(mask_blk, user_shard.T, item_shard, triples.T)  64.3 us

profile of v5, /device:TPU:1, one launch (start us, length us, event | category | flops | bytes accessed | tf_op | source)
XLA Modules:
  0.0 65.6 jit_solution(2423931780183014868)
XLA Ops:
  0.6 64.3 %shard_map.67 = (bf16[64,256]{1,0:T(8,128)(2,1)S(1)}, bf16[16,64]{1,0:T(8,128)(2,1)S(1)}, f32[8,128]{1,0:T(8,128)S(1)}) custom-call(s32[1024,1024]{1,0:T(8,128)} %mask_hbm.1, bf16[64,256]{1,0:T(8,128)(2,1)} %bitcast.4, bf16[16,64]{1,0:T(8,128)(2,1)} %item_hbm.1, s32[3,1024]{1,0:T(4,128)} %bitcast.5), custom_call_target="tpu_custom_call" | custom-call | tf_op jit(solution)/shard_map/pallas_call | solution.py:515
  64.9 0.6 shard_map.68

commit v6 on v5

--- a/solution.py
+++ b/solution.py
@@ -143,9 +143,6 @@
 
     def user_panel(layer):
         return columns(UAG, layer, range(4))
-
-    def item_panel(layer):
-        return jnp.concatenate([columns(IAG, layer, range(4)), columns(IAG, layer, range(4, 8))], axis=0)
 
     def arrive_both(kind, layer):
         for half in (0, 1):
@@ -267,20 +264,48 @@
                 send(stage, slot, buf.at[off], target(off))
             only(0)(lambda: send(stage, slot, buf.at[0], target(0)))
 
-        def item_columns(layer, user_rows, prepare=None):
-            def product(off):
-                cols = pl.ds(pl.multiple_of((yy + off) % 4 * 256, 256), 256)
-                if prepare is not None:
-                    prepare(cols)
-                return mm(user_rows, adj[:, cols], NN)
-
+        def in_halves(kind, layer, picks, rhs, dims):
+            def left(half):
+                arrive(layer_stage(kind, layer, half))
+                buf = slots[layer_stage(kind, layer, half)]
+                return jnp.concatenate(
+                    [jnp.concatenate([buf[idx] for idx in pick], axis=1) for pick in picks], axis=0)
+
+            first = left(0)
+            for off in DX:
+                chosen[off] = mm(first, rhs(off, 0), dims)
+            second = left(1)
+            return lambda off: chosen[off] + mm(second, rhs(off, 1), dims)
+
+        def item_columns(layer, prepare=None):
+            def cols(off):
+                return pl.ds(pl.multiple_of((yy + off) % 4 * 256, 256), 256)
+
+            def rhs(off, half):
+                return jnp.concatenate(
+                    [adj[pl.ds(k * 256 + half * LANES, LANES), cols(off)] for k in range(4)], axis=0)
+
+            def whole(off):
+                prepare(cols(off))
+                return mm(panel(EMB_USER), adj[:, cols(off)], NN)
+
+            product = whole if prepare else in_halves(UAG, layer - 1, (range(4),), rhs, NN)
             spread_halves(IRS, layer, pos, part_item, DY, product, lambda off: at_y(off, 1))
 
-        def user_products(layer, item_rows):
-            def product(off):
-                rows = pl.ds(pl.multiple_of((col + off) % 4 * 256, 256), 256)
-                return mm(item_rows, adj[rows, :], NT)
-
+        def user_products(layer):
+            def rows(off):
+                return pl.ds(pl.multiple_of((col + off) % 4 * 256, 256), 256)
+
+            def rhs(off, half):
+                return jnp.concatenate(
+                    [adj[rows(off), pl.ds(k * 256 + half * LANES, LANES)] for k in range(4)], axis=1)
+
+            def whole(off):
+                return mm(panel(EMB_ITEM_B), adj[rows(off), :], NT)
+
+            product = whole
+            if layer > 1:
+                product = in_halves(IAG, layer - 1, (range(4), range(4, 8)), rhs, NT)
             spread_halves(URS, layer, core * 4 + col, part_user, DX, product, lambda off: at_x(off, 1))
 
         @only(1)
@@ -380,9 +405,9 @@
                                 send(stage, mine, keep, (col, plane * 8 + (yy + dy) % 4 * 2 + which))
                 slots[stage][mine] = res
 
-        item_columns(1, panel(EMB_USER), prepare)
+        item_columns(1, prepare)
         arrive(EMB_ITEM_B)
-        user_products(1, panel(EMB_ITEM_B))
+        user_products(1)
 
         @only(1)
         def _():
@@ -398,17 +423,13 @@
                 step(1, half)
         for half in (0, 1):
             item_end(1, half)
-        arrive_both(UAG, 1)
-        item_columns(2, user_panel(1))
-        arrive_both(IAG, 1)
-        user_products(2, item_panel(1))
+        item_columns(2)
+        user_products(2)
         for step in (item_mid, user_end, item_end):
             for half in (0, 1):
                 step(2, half)
-        arrive_both(UAG, 2)
-        item_columns(3, user_panel(2))
-        arrive_both(IAG, 2)
-        user_products(3, item_panel(2))
+        item_columns(3)
+        user_products(3)
         for half in (0, 1):
             item_mid(3, half)
         for step in (user_end, item_end):

time: 65.6 us -> 65.2 us (level)
  no operation moved by 1% of the time
where the time goes in v6:
time: 65.2 us; the launch traced here: 65.1 us
  Pallas kernels  64.5 us (99%)
    pallas_call x1, Pallas kernels, device_body(): held = call(mask_blk, user_shard.T, item_shard, triples.T)  63.9 us

profile of v6, /device:TPU:1, one launch (start us, length us, event | category | flops | bytes accessed | tf_op | source)
XLA Modules:
  0.0 65.1 jit_solution(13860361407549500651)
XLA Ops:
  0.6 63.9 %shard_map.67 = (bf16[64,256]{1,0:T(8,128)(2,1)S(1)}, bf16[16,64]{1,0:T(8,128)(2,1)S(1)}, f32[8,128]{1,0:T(8,128)S(1)}) custom-call(s32[1024,1024]{1,0:T(8,128)} %mask_hbm.1, bf16[64,256]{1,0:T(8,128)(2,1)} %bitcast.4, bf16[16,64]{1,0:T(8,128)(2,1)} %item_hbm.1, s32[3,1024]{1,0:T(4,128)} %bitcast.5), custom_call_target="tpu_custom_call" | custom-call | tf_op jit(solution)/shard_map/pallas_call | solution.py:536
  64.5 0.6 shard_map.68

commit v7 on v6

--- a/solution.py
+++ b/solution.py
@@ -9,7 +9,7 @@
 
 LAYERS = 3
 LANES = 128
-LOADS = 8
+LOADS = 16
 F32 = jnp.float32
 BF16 = jnp.bfloat16
 I32 = jnp.int32

time: 65.2 us -> 65.1 us (level)
  no operation moved by 1% of the time
where the time goes in v7:
time: 65.1 us; the launch traced here: 65 us
  Pallas kernels  64.4 us (99%)
    pallas_call x1, Pallas kernels, device_body(): held = call(mask_blk, user_shard.T, item_shard, triples.T)  63.7 us

profile of v7, /device:TPU:1, one launch (start us, length us, event | category | flops | bytes accessed | tf_op | source)
XLA Modules:
  0.0 65.0 jit_solution(8650381403341440362)
XLA Ops:
  0.6 63.7 %shard_map.67 = (bf16[64,256]{1,0:T(8,128)(2,1)S(1)}, bf16[16,64]{1,0:T(8,128)(2,1)S(1)}, f32[8,128]{1,0:T(8,128)S(1)}) custom-call(s32[1024,1024]{1,0:T(8,128)} %mask_hbm.1, bf16[64,256]{1,0:T(8,128)(2,1)} %bitcast.4, bf16[16,64]{1,0:T(8,128)(2,1)} %item_hbm.1, s32[3,1024]{1,0:T(4,128)} %bitcast.5), custom_call_target="tpu_custom_call" | custom-call | tf_op jit(solution)/shard_map/pallas_call | solution.py:536
  64.4 0.6 shard_map.68

commit v8 on v7

--- a/solution.py
+++ b/solution.py
@@ -346,14 +346,10 @@
         def prepare(cols):
             si = si_row[:, cols]
 
-            def build(blk, carry):
-                base = pl.multiple_of(blk * 128, 128)
-                for k in range(8):
-                    rows = pl.ds(pl.multiple_of(base + k * 16, 16), 16)
-                    adj[rows, cols] = (mask_su[rows, cols] * jnp.concatenate([si, si], axis=0)).astype(BF16)
-                return carry
-
-            lax.fori_loop(0, 8, build, 0)
+            si2 = jnp.concatenate([si, si], axis=0)
+            for k in range(64):
+                rows = slice(k * 16, (k + 1) * 16)
+                adj[rows, cols] = (mask_su[rows, cols] * si2).astype(BF16)
 
         def item_mid(layer, half):
             @only(1)

time: 65.1 us -> 65.2 us (level)
  no operation moved by 1% of the time
where the time goes in v8:
time: 65.2 us; the launch traced here: 65.1 us
  Pallas kernels  64.5 us (99%)
    pallas_call x1, Pallas kernels, device_body(): held = call(mask_blk, user_shard.T, item_shard, triples.T)  63.9 us

profile of v8, /device:TPU:1, one launch (start us, length us, event | category | flops | bytes accessed | tf_op | source)
XLA Modules:
  0.0 65.1 jit_solution(1848554522904504896)
XLA Ops:
  0.6 63.9 %shard_map.67 = (bf16[64,256]{1,0:T(8,128)(2,1)S(1)}, bf16[16,64]{1,0:T(8,128)(2,1)S(1)}, f32[8,128]{1,0:T(8,128)S(1)}) custom-call(s32[1024,1024]{1,0:T(8,128)} %mask_hbm.1, bf16[64,256]{1,0:T(8,128)(2,1)} %bitcast.4, bf16[16,64]{1,0:T(8,128)(2,1)} %item_hbm.1, s32[3,1024]{1,0:T(4,128)} %bitcast.5), custom_call_target="tpu_custom_call" | custom-call | tf_op jit(solution)/shard_map/pallas_call | solution.py:532
  64.5 0.6 shard_map.68
